TPU v7x, 8 devices: a whole 2x2x1 slice. The times are simulated.
8 devices in a mesh: rep: 2 (over z, y), data: 4 (over x, core).
Axes of the slice: x: 2, y: 2, z: 1, core: 2. Of those that a mesh axis runs over, the one named last changes fastest.
Arguments:
- W_in: float32 [12288, 768], P('rep'), parts along dimension 0
- W1: float32 [6, 768, 3072], P('rep'), parts along dimension 0
- W2: float32 [6, 3072, 768], P('rep'), parts along dimension 0
- m_in: float32 [12288, 768], P('rep'), parts along dimension 0
- v_in: float32 [12288, 768], P('rep'), parts along dimension 0
- m1: float32 [6, 768, 3072], P('rep'), parts along dimension 0
- v1: float32 [6, 768, 3072], P('rep'), parts along dimension 0
- m2: float32 [6, 3072, 768], P('rep'), parts along dimension 0
- v2: float32 [6, 3072, 768], P('rep'), parts along dimension 0
- X0: bfloat16 [16384, 6144], P(('rep', 'data')), parts along dimension 0
- Y0: bfloat16 [16384, 768], P(('rep', 'data')), parts along dimension 0
- X1: bfloat16 [16384, 6144], P(('rep', 'data')), parts along dimension 0
- Y1: bfloat16 [16384, 768], P(('rep', 'data')), parts along dimension 0
Outputs:
- output 1: float32 [12288, 768], P('rep'), parts along dimension 0
- output 2: float32 [6, 768, 3072], P('rep'), parts along dimension 0
- output 3: float32 [6, 3072, 768], P('rep'), parts along dimension 0
- output 4: float32 [12288, 768], P('rep'), parts along dimension 0
- output 5: float32 [12288, 768], P('rep'), parts along dimension 0
- output 6: float32 [6, 768, 3072], P('rep'), parts along dimension 0
- output 7: float32 [6, 768, 3072], P('rep'), parts along dimension 0
- output 8: float32 [6, 3072, 768], P('rep'), parts along dimension 0
- output 9: float32 [6, 3072, 768], P('rep'), parts along dimension 0
- output 10: float32 [16384], P(('rep', 'data')), parts along dimension 0
- output 11: float32 [16384, 768], P(('rep', 'data')), parts along dimension 0
There are 2 independent parts. A program takes and returns all parts, laid end to end along the dimension named above; each array names one.
All inputs are finite; a program needn't handle non-finite values.
Results may differ from a plain program's by a relative error of at most 0.0144442.
Values are sent between devices in bfloat16 or wider.
A program may use at most 2 GiB of HBM per device.

v0:
```python
import jax
import jax.numpy as jnp
from jax import lax
from jax.sharding import PartitionSpec as P

BETA1 = 0.9
BETA2 = 0.999
BC1 = 1.0 / (1.0 - BETA1 ** 10)
BC2 = 1.0 / (1.0 - BETA2 ** 10)
EPS = 1e-12
WD = 0.01
ETA = 0.05
R2 = 0.7071067811865476
R2PI = 0.3989422804014327
BF = jnp.bfloat16
F32 = jnp.float32


def gelu_grad(a):
    return 0.5 * (1.0 + lax.erf(a * R2)) + a * jnp.exp(-0.5 * a * a) * R2PI


def lamb(w, g, m, v):
    m2 = BETA1 * m + (1.0 - BETA1) * g
    v2 = BETA2 * v + (1.0 - BETA2) * g * g
    u = BC1 * m2 / (jnp.sqrt(BC2 * v2) + EPS) + WD * w
    r = jnp.sqrt(jnp.sum(w * w)) / jnp.sqrt(jnp.sum(u * u))
    return w - ETA * r * u, m2, v2


def group_sum(g, p):
    rows, cols = g.shape
    got = lax.all_to_all(g, 'data', 0, 0, tiled=True).reshape(p, rows // p, cols)
    s = jnp.sum(got, axis=0, dtype=F32).astype(BF)
    return lax.all_gather(s, 'data', axis=0, tiled=True).astype(F32)


def forward(wib, w1b, w2b, x):
    h = jnp.dot(x, wib, preferred_element_type=F32)
    for l in range(len(w1b)):
        s = jax.nn.gelu(jnp.dot(h.astype(BF), w1b[l], preferred_element_type=F32), approximate=False).astype(BF)
        h = h + jnp.dot(s, w2b[l], preferred_element_type=F32)
    return h


def stacked(ups, k):
    return jnp.stack([u[k] for u in ups])


def solution(mesh):
    p = mesh.shape['data']

    def step(wi, w1, w2, mi, vi, m1, v1, m2, v2, x0, y0, x1, y1):
        nl = w1.shape[0]
        d = wi.shape[1]
        scale = 1.0 / (x0.shape[0] * p * d)
        wib = wi.astype(BF)
        w1b = [w1[l].astype(BF) for l in range(nl)]
        w2b = [w2[l].astype(BF) for l in range(nl)]
        h = jnp.dot(x0, wib, preferred_element_type=F32)
        saved = []
        for l in range(nl):
            a = jnp.dot(h.astype(BF), w1b[l], preferred_element_type=F32)
            s = jax.nn.gelu(a, approximate=False).astype(BF)
            saved.append((h.astype(BF), a, s))
            h = h + jnp.dot(s, w2b[l], preferred_element_type=F32)
        g = (h - y0.astype(F32)) * scale
        dw1 = [None] * nl
        dw2 = [None] * nl
        for l in reversed(range(nl)):
            hb, a, s = saved[l]
            gb = g.astype(BF)
            dw2[l] = jnp.dot(s.T, gb, preferred_element_type=F32).astype(BF)
            e = (jnp.dot(gb, w2b[l].T, preferred_element_type=F32) * gelu_grad(a)).astype(BF)
            dw1[l] = jnp.dot(hb.T, e, preferred_element_type=F32).astype(BF)
            g = g + jnp.dot(e, w1b[l].T, preferred_element_type=F32)
        dwi = jnp.dot(x0.T, g.astype(BF), preferred_element_type=F32).astype(BF)
        s1 = [None] * nl
        s2 = [None] * nl
        for l in reversed(range(nl)):
            s2[l] = group_sum(dw2[l], p)
            s1[l] = group_sum(dw1[l], p)
        si = group_sum(dwi, p)
        wi_n, mi_n, vi_n = lamb(wi, si, mi, vi)
        up1 = [lamb(w1[l], s1[l], m1[l], v1[l]) for l in range(nl)]
        up2 = [lamb(w2[l], s2[l], m2[l], v2[l]) for l in range(nl)]
        h1 = forward(wi_n.astype(BF), [u[0].astype(BF) for u in up1], [u[0].astype(BF) for u in up2], x1)
        loss = jnp.sum((h1 - y1.astype(F32)) ** 2, axis=-1) / (2.0 * d)
        return (wi_n, stacked(up1, 0), stacked(up2, 0), mi_n, vi_n,
                stacked(up1, 1), stacked(up1, 2), stacked(up2, 1), stacked(up2, 2), loss, h1)

    w2s = P('rep', None)
    w3s = P('rep', None, None)
    ts = P(('rep', 'data'), None)
    return jax.shard_map(step, mesh=mesh,
                         in_specs=(w2s, w3s, w3s, w2s, w2s, w3s, w3s, w3s, w3s, ts, ts, ts, ts),
                         out_specs=(w2s, w3s, w3s, w2s, w2s, w3s, w3s, w3s, w3s, P(('rep', 'data')), ts),
                         check_vma=False)
```

profile of v0, /device:TPU:0, one launch (start us, length us, event | category | flops | bytes accessed | tf_op | source)
XLA Modules:
  0.0 1784.1 jit_solution(2489968539338999431)
XLA Ops:
  7.2 25.9 %fusion.112 = f32[2048,768]{1,0:T(8,128)S(1)} fusion(bf16[2048,6144]{1,0:T(8,128)(2,1)} %param.22, f32[6144,768]{1,0:T(8,128)} %param.13), kind=kOutput, calls=%fused_computation.222 | convolution fusion | flops 19332071424 | bytes 50331648 | tf_op jit(solution)/shard_map/dot_general | solution.py:60
  33.1 67.4 %fusion.2 = (bf16[2048,3072]{1,0:T(8,128)(2,1)}, f32[2048,3072]{1,0:T(8,128)}) fusion(f32[3,768,3072]{2,1,0:T(8,128)} %param.14, f32[2048,768]{1,0:T(8,128)S(1)} %fusion.112), kind=kOutput, calls=%fused_computation.18 | convolution fusion | flops 10074193920 | bytes 48758784 | tf_op jit(solution)/shard_map/dot_general | solution.py:63
  100.5 16.3 convolution_add_fusion.3
  116.8 67.1 %fusion.5 = (bf16[2048,3072]{1,0:T(8,128)(2,1)}, f32[2048,3072]{1,0:T(8,128)}) fusion(f32[3,768,3072]{2,1,0:T(8,128)} %param.14, f32[2048,768]{1,0:T(8,128)S(1)} %convolution_add_fusion.3), kind=kOutput, calls=%fused_computation.21 | convolution fusion | flops 10074193920 | bytes 48758784 | tf_op jit(solution)/shard_map/dot_general | solution.py:63
  184.0 15.9 convolution_add_fusion.2
  199.9 67.0 %fusion.8 = (bf16[2048,3072]{1,0:T(8,128)(2,1)}, f32[2048,3072]{1,0:T(8,128)}) fusion(f32[3,768,3072]{2,1,0:T(8,128)} %param.14, f32[2048,768]{1,0:T(8,128)S(1)} %convolution_add_fusion.2), kind=kOutput, calls=%fused_computation.24 | convolution fusion | flops 10074193920 | bytes 48758784 | tf_op jit(solution)/shard_map/dot_general | solution.py:63
  266.9 17.5 subtract_multiply_fusion
  284.3 25.3 %fusion.14 = bf16[2048,3072]{1,0:T(8,128)(2,1)} fusion(f32[2048,3072]{1,0:T(8,128)} %get-tuple-element.85, f32[3,3072,768]{2,1,0:T(8,128)} %param.15, f32[2048,768]{1,0:T(8,128)} %subtract_multiply_fusion), kind=kOutput, calls=%fused_computation.30 | convolution fusion | flops 9728163840 | bytes 48758784 | tf_op jit(solution)/shard_map/dot_general | solution.py:74
  309.6 17.4 convolution_add_fusion.1
  327.0 25.6 %fusion.20 = bf16[2048,3072]{1,0:T(8,128)(2,1)} fusion(f32[2048,3072]{1,0:T(8,128)} %get-tuple-element.83, f32[3,3072,768]{2,1,0:T(8,128)} %param.15, f32[2048,768]{1,0:T(8,128)} %convolution_add_fusion.1), kind=kOutput, calls=%fused_computation.36 | convolution fusion | flops 9728163840 | bytes 48758784 | tf_op jit(solution)/shard_map/dot_general | solution.py:74
  352.6 18.4 %convolution_add_fusion = f32[2048,768]{1,0:T(8,128)} fusion(f32[2048,768]{1,0:T(8,128)} %convolution_add_fusion.1, bf16[2048,3072]{1,0:T(8,128)(2,1)} %fusion.20, f32[3,768,3072]{2,1,0:T(8,128)} %param.14), kind=kOutput, calls=%fused_computation.258 | convolution fusion | flops 9665249280 | bytes 29884416 | tf_op jit(solution)/shard_map/dot_general | solution.py:76
  370.9 23.3 %fusion.26 = bf16[2048,3072]{1,0:T(8,128)(2,1)S(1)} fusion(f32[2048,3072]{1,0:T(8,128)} %get-tuple-element.81, f32[3,3072,768]{2,1,0:T(8,128)} %param.15, f32[2048,768]{1,0:T(8,128)} %convolution_add_fusion), kind=kOutput, calls=%fused_computation.42 | convolution fusion | flops 9728163840 | bytes 48758784 | tf_op jit(solution)/shard_map/dot_general | solution.py:74
  409.9 58.2 %all_to_all.63 = bf16[4,192,3072]{2,1,0:T(8,128)(2,1)} all-to-all(bf16[4,192,3072]{2,1,0:T(8,128)(2,1)S(1)} %bitcast.318), channel_id=1, replica_groups=mesh['rep'=2,'data'=4] {'data'}, dimensions={0} | all-to-all | bytes 9437184 | tf_op jit(solution)/shard_map/all_to_all | solution.py:33
  472.7 14.9 convolution_convert_fusion.5
  487.6 69.7 %all_to_all.64 = bf16[4,192,3072]{2,1,0:T(8,128)(2,1)} all-to-all(bf16[4,192,3072]{2,1,0:T(8,128)(2,1)S(1)} %bitcast.315), channel_id=1, replica_groups=mesh['rep'=2,'data'=4] {'data'}, dimensions={0} | all-to-all | bytes 9437184 | tf_op jit(solution)/shard_map/all_to_all | solution.py:33
  561.9 15.3 convolution_convert_fusion.4
  577.2 68.4 %all_to_all.65 = bf16[4,192,3072]{2,1,0:T(8,128)(2,1)} all-to-all(bf16[4,192,3072]{2,1,0:T(8,128)(2,1)S(1)} %bitcast.316), channel_id=1, replica_groups=mesh['rep'=2,'data'=4] {'data'}, dimensions={0} | all-to-all | bytes 9437184 | tf_op jit(solution)/shard_map/all_to_all | solution.py:33
  650.2 15.1 convolution_convert_fusion.3
  665.3 68.6 %all_to_all.66 = bf16[4,768,768]{2,1,0:T(8,128)(2,1)} all-to-all(bf16[4,768,768]{2,1,0:T(8,128)(2,1)S(1)} %bitcast.319), channel_id=1, replica_groups=mesh['rep'=2,'data'=4] {'data'}, dimensions={0} | all-to-all | bytes 9437184 | tf_op jit(solution)/shard_map/all_to_all | solution.py:33
  738.3 14.9 convolution_convert_fusion.2
  753.3 68.7 %all_to_all.67 = bf16[4,768,768]{2,1,0:T(8,128)(2,1)} all-to-all(bf16[4,768,768]{2,1,0:T(8,128)(2,1)S(1)} %bitcast.317), channel_id=1, replica_groups=mesh['rep'=2,'data'=4] {'data'}, dimensions={0} | all-to-all | bytes 9437184 | tf_op jit(solution)/shard_map/all_to_all | solution.py:33
  826.4 16.4 convolution_convert_fusion.1
  848.1 16.8 add_convert_fusion
  864.9 25.6 %convolution_convert_fusion = bf16[768,6144]{1,0:T(8,128)(2,1)} fusion(bf16[2048,768]{1,0:T(8,128)(2,1)S(1)} %add_convert_fusion, bf16[2048,6144]{1,0:T(8,128)(2,1)} %param.22), kind=kOutput, calls=%fused_computation.164 | convolution fusion | flops 19332071424 | bytes 37748736 | tf_op jit(solution)/shard_map/dot_general | solution.py:77
  920.4 18.8 %copy.31 = f32[6144,768]{0,1:T(8,128)} copy(f32[6144,768]{1,0:T(8,128)} %param.13) | data formatting | bytes 37748736 | tf_op args[0]
  950.9 18.7 %copy.26 = f32[6144,768]{0,1:T(8,128)} copy(f32[6144,768]{1,0:T(8,128)} %param.16) | data formatting | bytes 37748736 | tf_op args[3]
  969.6 18.6 %copy.29 = f32[6144,768]{0,1:T(8,128)} copy(f32[6144,768]{1,0:T(8,128)} %param.17) | data formatting | bytes 37748736 | tf_op args[4]
  1018.2 27.1 %all-to-all-done = bf16[4,1536,768]{1,2,0:T(8,128)(2,1)} async-done(((bf16[4,1536,768]{1,2,0:T(8,128)(2,1)}), bf16[4,1536,768]{1,2,0:T(8,128)(2,1)}, u32[]{:S(2)}, u32[]{:S(2)}) %all-to-all-start) | async-done | bytes 9437216 | tf_op jit(solution)/shard_map/all_to_all | solution.py:33
  1052.6 60.5 %multiply_reduce_fusion.7 = (f32[]{:T(128)}, f32[768,3072]{1,0:T(8,128)}, f32[]{:T(128)}, f32[768,3072]{1,0:T(8,128)}, f32[]{:T(128)}, /*index=5*/f32[768,3072]{...) fusion(f32[3,768,3072]{2,1,0:T(8,128)} %param.14, ...), kind=kLoop, calls=%fused_computation.221 | loop fusion | flops 113246208 | bytes 184025104 | tf_op jit(solution)/shard_map/reduce_sum | solution.py:27
  1113.9 63.2 %multiply_reduce_fusion.4 = (f32[]{:T(128)}, f32[3072,768]{1,0:T(8,128)}, f32[]{:T(128)}, f32[3072,768]{1,0:T(8,128)}, f32[]{:T(128)}, /*index=5*/f32[3072,768]{...) fusion(f32[3,3072,768]{2,1,0:T(8,128)} %param.15, ...), kind=kLoop, calls=%fused_computation.218 | loop fusion | flops 113246208 | bytes 184025104 | tf_op jit(solution)/shard_map/reduce_sum | solution.py:27
  1180.6 28.1 %fusion.166 = (f32[1,3072,768]{2,1,0:T(8,128)}, f32[1,3072,768]{2,1,0:T(8,128)}, f32[1,3072,768]{2,1,0:T(8,128)}) fusion(f32[3072,768]{1,0:T(8,128)} %get-tuple-element.40, f32[]{:T(128)S(6)} %mul.562, f32[3,3072,768]{2,1,0:T(8,128)} %param.15, f32[3072,768]{1,0:T(8,128)} %get-tuple-element.55, f32[]{:T(128)S(6)} %mul.577, ...), kind=kLoop, calls=%fused_computation.265 | loop fusion | flops 14155776 | bytes 84934672 | tf_op jit(solution)/shard_map/stack | solution.py:47
  1208.7 20.8 %pad_maximum_fusion.1 = f32[3,3072,768]{2,1,0:T(8,128)} fusion(f32[1,3072,768]{2,1,0:T(8,128)} %get-tuple-element.76, f32[1,3072,768]{2,1,0:T(8,128)} %get-tuple-element.75, f32[1,3072,768]{2,1,0:T(8,128)} %get-tuple-element.74), kind=kLoop, calls=%fused_computation.10 | loop fusion | flops 14155776 | bytes 56623104 | tf_op jit(solution)/shard_map/stack | solution.py:47
  1229.5 29.2 %fusion.165 = (f32[1,768,3072]{2,1,0:T(8,128)}, f32[1,768,3072]{2,1,0:T(8,128)}, f32[1,768,3072]{2,1,0:T(8,128)}) fusion(f32[768,3072]{1,0:T(8,128)} %get-tuple-element.46, f32[]{:T(128)S(6)} %mul.517, f32[3,768,3072]{2,1,0:T(8,128)} %param.14, f32[768,3072]{1,0:T(8,128)} %get-tuple-element.59, f32[]{:T(128)S(6)} %mul.532, ...), kind=kLoop, calls=%fused_computation.264 | loop fusion | flops 14155776 | bytes 84934672 | tf_op jit(solution)/shard_map/stack | solution.py:47
  1258.7 22.9 %pad_maximum_fusion = f32[3,768,3072]{2,1,0:T(8,128)} fusion(f32[1,768,3072]{2,1,0:T(8,128)} %get-tuple-element.79, f32[1,768,3072]{2,1,0:T(8,128)} %get-tuple-element.78, f32[1,768,3072]{2,1,0:T(8,128)} %get-tuple-element.77), kind=kLoop, calls=%fused_computation.9 | loop fusion | flops 14155776 | bytes 56623104 | tf_op jit(solution)/shard_map/stack | solution.py:47
  1281.6 39.5 %pad_maximum_fusion.4 = (f32[3,3072,768]{2,1,0:T(8,128)}, f32[3,3072,768]{2,1,0:T(8,128)}) fusion(f32[1,3072,768]{2,1,0:T(8,128)} %get-tuple-element.69, f32[1,3072,768]{2,1,0:T(8,128)} %get-tuple-element.68, f32[1,3072,768]{2,1,0:T(8,128)} %get-tuple-element.71, f32[1,3072,768]{2,1,0:T(8,128)} %get-tuple-element.67, f32[1,3072,768]{2,1,0:T(8,128)} %get-tuple-element.66, ...), kind=kLoop, calls=%fused_computation.13 | loop fusion | flops 28311552 | bytes 113246208 | tf_op jit(solution)/shard_map/stack | solution.py:47
  1321.2 31.4 %pad_maximum_fusion.2 = (f32[3,768,3072]{2,1,0:T(8,128)}, f32[3,768,3072]{2,1,0:T(8,128)}) fusion(f32[1,768,3072]{2,1,0:T(8,128)} %get-tuple-element.65, f32[1,768,3072]{2,1,0:T(8,128)} %get-tuple-element.64, f32[1,768,3072]{2,1,0:T(8,128)} %get-tuple-element.73, f32[1,768,3072]{2,1,0:T(8,128)S(1)} %bitcast.311, f32[1,768,3072]{2,1,0:T(8,128)S(1)} %bitcast.309, ...), kind=kLoop, calls=%fused_computation.11 | loop fusion | flops 28311552 | bytes 113246208 | tf_op jit(solution)/shard_map/stack | solution.py:47
  1352.7 35.5 %multiply_reduce_fusion = (f32[]{:T(128)}, f32[6144,768]{0,1:T(8,128)}, f32[6144,768]{0,1:T(8,128)}) fusion(f32[6144,768]{0,1:T(8,128)} %copy.31, bf16[6144,768]{0,1:T(8,128)(2,1)} %all-gather.8.cloned.1.call-done, f32[6144,768]{0,1:T(8,128)} %copy.26, f32[6144,768]{0,1:T(8,128)} %copy.29), kind=kLoop, calls=%fused_computation.146 | loop fusion | flops 75497472 | bytes 103809024 | tf_op jit(solution)/shard_map/reduce_sum | solution.py:27
  1388.9 18.6 %copy.34 = f32[6144,768]{1,0:T(8,128)} copy(f32[6144,768]{0,1:T(8,128)} %get-tuple-element.52) | data formatting | bytes 37748736
  1407.5 18.6 %copy.35 = f32[6144,768]{1,0:T(8,128)} copy(f32[6144,768]{0,1:T(8,128)} %get-tuple-element.53) | data formatting | bytes 37748736
  1426.1 25.3 %multiply_subtract_fusion = f32[6144,768]{0,1:T(8,128)} fusion(f32[6144,768]{0,1:T(8,128)} %copy.31, f32[]{:T(128)S(6)} %mul.502, f32[6144,768]{0,1:T(8,128)} %get-tuple-element.53, f32[6144,768]{0,1:T(8,128)} %get-tuple-element.52), kind=kLoop, calls=%fused_computation.145 | loop fusion | flops 37748736 | bytes 75497472 | tf_op jit(solution)/shard_map/sub | solution.py:28
  1451.4 18.7 %copy.33 = f32[6144,768]{1,0:T(8,128)} copy(f32[6144,768]{0,1:T(8,128)} %multiply_subtract_fusion) | data formatting | bytes 37748736
  1470.2 27.4 %fusion.110 = f32[768,2048]{1,0:T(8,128)} fusion(bf16[2048,6144]{1,0:T(8,128)(2,1)} %param.24, f32[6144,768]{0,1:T(8,128)} %multiply_subtract_fusion), kind=kOutput, calls=%fused_computation.214 | convolution fusion | flops 19332071424 | bytes 50331648 | tf_op jit(solution)/shard_map/dot_general | solution.py:39
  1497.5 69.9 %fusion.337 = bf16[2048,3072]{1,0:T(8,128)(2,1)} fusion(f32[768,2048]{1,0:T(8,128)} %fusion.110, f32[768,3072]{1,0:T(8,128)S(1)} %bitcast.307, f32[3,768,3072]{2,1,0:T(8,128)} %param.14, f32[]{:T(128)S(6)} %mul.517), kind=kOutput, calls=%fused_computation.45.clone.clone.clone.clone.2 | convolution fusion | flops 10079698944 | bytes 37748740 | tf_op jit(solution)/shard_map/dot_general | solution.py:41
  1567.4 20.5 %bitcast_add_fusion = f32[2048,768]{0,1:T(8,128)} fusion(f32[768,2048]{1,0:T(8,128)} %fusion.110, f32[3072,768]{1,0:T(8,128)} %get-tuple-element.40, f32[3,3072,768]{2,1,0:T(8,128)} %param.15, f32[]{:T(128)S(6)} %mul.562, bf16[2048,3072]{1,0:T(8,128)(2,1)} %fusion.337), kind=kOutput, calls=%fused_computation.224 | convolution fusion | flops 9672327168 | bytes 44040196 | tf_op jit(solution)/shard_map/dot_general | solution.py:42
  1587.9 70.1 %fusion.344 = bf16[2048,3072]{1,0:T(8,128)(2,1)} fusion(f32[2048,768]{0,1:T(8,128)} %bitcast_add_fusion, f32[768,3072]{1,0:T(8,128)} %get-tuple-element.59, f32[3,768,3072]{2,1,0:T(8,128)} %param.14, f32[]{:T(128)S(6)} %mul.532), kind=kOutput, calls=%fused_computation.48.clone.clone.clone.clone.2 | convolution fusion | flops 10081271808 | bytes 37748740 | tf_op jit(solution)/shard_map/dot_general | solution.py:41
  1658.0 20.5 %fusion.147 = f32[2048,768]{0,1:T(8,128)} fusion(f32[2048,768]{0,1:T(8,128)} %bitcast_add_fusion, f32[3072,768]{1,0:T(8,128)} %get-tuple-element.55, f32[3,3072,768]{2,1,0:T(8,128)} %param.15, f32[]{:T(128)S(6)} %mul.577, bf16[2048,3072]{1,0:T(8,128)(2,1)} %fusion.344), kind=kOutput, calls=%fused_computation.256 | convolution fusion | flops 9672327168 | bytes 44040196 | tf_op jit(solution)/shard_map/dot_general | solution.py:42
  1678.5 70.5 %fusion.160.clone.5 = bf16[2048,3072]{1,0:T(8,128)(2,1)} fusion(f32[2048,768]{0,1:T(8,128)} %fusion.147, f32[768,3072]{1,0:T(8,128)} %get-tuple-element.61, f32[3,768,3072]{2,1,0:T(8,128)} %param.14, f32[]{:T(128)S(6)} %mul.547), kind=kOutput, calls=%fused_computation.51.clone.clone.clone.clone.clone.clone.2 | convolution fusion | flops 10081271808 | bytes 37748740 | tf_op jit(solution)/shard_map/dot_general | solution.py:41
  1749.0 20.9 %multiply_reduce_fusion.8 = (f32[2048]{0:T(1024)S(1)}, f32[2048,768]{0,1:T(8,128)}) fusion(bf16[2048,768]{0,1:T(8,128)(2,1)S(1)} %copy-done.1, f32[2048,768]{0,1:T(8,128)} %fusion.147, f32[3072,768]{1,0:T(8,128)} %get-tuple-element.57, f32[]{:T(128)S(6)} %mul.592, f32[3,3072,768]{2,1,0:T(8,128)} %param.15, bf16[2048,3072]{1,0:T(8,128)(2,1)} %fusion.160.clone.5), kind=kOutput, calls=%fused_computation.226 | convolution fusion | flops 9678616576 | bytes 47194116 | tf_op jit(solution)/shard_map/dot_general | solution.py:42
  (81 shorter events, 125.0 us)
Async XLA Ops:
  7.2 1045.4 %all-gather.10.cloned.1.call-start = ((), (), s32[]{:S(2)}) async-start(), calls=%async_computation.8 | async-start | bytes 5898240 | tf_op jit(solution)/shard_map/all_gather | solution.py:35
  33.1 67.4 %copy-start.6 = (f32[2048,768]{1,0:T(8,128)}, f32[2048,768]{1,0:T(8,128)S(1)}, u32[]{:S(2)}) copy-start(f32[2048,768]{1,0:T(8,128)S(1)} %fusion.112) | copy-start | bytes 18874372
  116.8 67.2 %copy-start.5 = (f32[2048,768]{1,0:T(8,128)}, f32[2048,768]{1,0:T(8,128)S(1)}, u32[]{:S(2)}) copy-start(f32[2048,768]{1,0:T(8,128)S(1)} %convolution_add_fusion.3) | copy-start | bytes 18874372
  199.8 67.0 %copy-start.4 = (f32[2048,768]{1,0:T(8,128)}, f32[2048,768]{1,0:T(8,128)S(1)}, u32[]{:S(2)}) copy-start(f32[2048,768]{1,0:T(8,128)S(1)} %convolution_add_fusion.2) | copy-start | bytes 18874372
  199.9 67.0 %copy-start.2 = (bf16[2048,768]{1,0:T(8,128)(2,1)S(1)}, bf16[2048,768]{1,0:T(8,128)(2,1)}, u32[]{:S(2)}) copy-start(bf16[2048,768]{1,0:T(8,128)(2,1)} %param.23) | copy-start | bytes 9437188
  284.3 25.3 %copy-start.7 = (f32[2048,768]{1,0:T(8,128)S(1)}, f32[2048,768]{1,0:T(8,128)}, u32[]{:S(2)}) copy-start(f32[2048,768]{1,0:T(8,128)} %subtract_multiply_fusion) | copy-start | bytes 18874372
  352.6 46.4 %slice-start.9 = ((s8[6291456]{0:T(1024)(128)(4,1)}), s8[4194304]{0:T(1024)(128)(4,1)S(1)}, s32[]{:S(2)}) async-start(s8[6291456]{0:T(1024)(128)(4,1)} %bitcast.320), calls=%async_computation.23 | async-start | bytes 8388608
  370.9 28.1 %slice-start.10 = ((s8[6291456]{0:T(1024)(128)(4,1)}), s8[2097152]{0:T(1024)(128)(4,1)S(1)}, s32[]{:S(2)}) async-start(s8[6291456]{0:T(1024)(128)(4,1)} %bitcast.320), calls=%async_computation.24 | async-start | bytes 4194304
  394.2 4.8 copy-start.3
  472.7 579.9 %all-gather.12.cloned.1.call-start = ((), (), s32[]{:S(2)}) async-start(), calls=%async_computation.9 | async-start | bytes 5898240 | tf_op jit(solution)/shard_map/all_gather | solution.py:35
  561.9 490.7 %all-gather.14.cloned.1.call-start = ((), (), s32[]{:S(2)}) async-start(), calls=%async_computation.10 | async-start | bytes 5898240 | tf_op jit(solution)/shard_map/all_gather | solution.py:35
  650.2 463.7 %all-gather.16.cloned.1.call-start = ((), (), s32[]{:S(2)}) async-start(), calls=%async_computation.11 | async-start | bytes 5898240 | tf_op jit(solution)/shard_map/all_gather | solution.py:35
  738.3 375.6 %all-gather.18.cloned.1.call-start = ((), (), s32[]{:S(2)}) async-start(), calls=%async_computation.12 | async-start | bytes 5898240 | tf_op jit(solution)/shard_map/all_gather | solution.py:35
  842.8 67.3 %all-to-all-start.6 = ((bf16[4,768,768]{2,1,0:T(8,128)(2,1)}), bf16[4,768,768]{2,1,0:T(8,128)(2,1)}, u32[]{:S(2)}, u32[]{:S(2)}) async-start(bf16[4,768,768]{2,1,0:T(8,128)(2,1)} %bitcast.314), calls=%async_computation.6 | async-start | bytes 9437184 | tf_op jit(solution)/shard_map/all_to_all | solution.py:33
  910.1 135.2 %all-to-all-start = ((bf16[4,1536,768]{1,2,0:T(8,128)(2,1)}), bf16[4,1536,768]{1,2,0:T(8,128)(2,1)}, u32[]{:S(2)}, u32[]{:S(2)}) async-start(bf16[4,1536,768]{1,2,0:T(8,128)(2,1)} %bitcast.312), calls=%async_computation | async-start | bytes 18874368 | tf_op jit(solution)/shard_map/all_to_all | solution.py:33
  915.9 198.0 %all-gather.20.cloned.1.call-start = ((), (), s32[]{:S(2)}) async-start(), calls=%async_computation.13 | async-start | bytes 5898240 | tf_op jit(solution)/shard_map/all_gather | solution.py:35
  920.4 432.3 %all-gather.8.cloned.1.call-start = ((), (), s32[]{:S(2)}) async-start(), calls=%async_computation.7 | async-start | bytes 11796480 | tf_op jit(solution)/shard_map/all_gather | solution.py:35
  988.3 26.9 %copy-start = (bf16[2048,768]{1,0:T(8,128)(2,1)S(1)}, bf16[2048,768]{1,0:T(8,128)(2,1)}, u32[]{:S(2)}) copy-start(bf16[2048,768]{1,0:T(8,128)(2,1)} %param.25) | copy-start | bytes 9437188
  1258.7 62.4 %slice-start.3 = ((s8[9437184]{0:T(1024)(128)(4,1)}), s8[4194304]{0:T(1024)(128)(4,1)S(1)}, s32[]{:S(2)}) async-start(s8[9437184]{0:T(1024)(128)(4,1)} %bitcast.308), calls=%async_computation.17 | async-start | bytes 8388608
  1258.7 62.4 %slice-start.6 = ((s8[9437184]{0:T(1024)(128)(4,1)}), s8[4194304]{0:T(1024)(128)(4,1)S(1)}, s32[]{:S(2)}) async-start(s8[9437184]{0:T(1024)(128)(4,1)} %bitcast.310), calls=%async_computation.20 | async-start | bytes 8388608
  1281.6 39.5 %slice-start.4 = ((s8[9437184]{0:T(1024)(128)(4,1)}), s8[4194304]{0:T(1024)(128)(4,1)S(1)}, s32[]{:S(2)}) async-start(s8[9437184]{0:T(1024)(128)(4,1)} %bitcast.308), calls=%async_computation.18 | async-start | bytes 8388608
  1281.6 39.6 %slice-start.7 = ((s8[9437184]{0:T(1024)(128)(4,1)}), s8[4194304]{0:T(1024)(128)(4,1)S(1)}, s32[]{:S(2)}) async-start(s8[9437184]{0:T(1024)(128)(4,1)} %bitcast.310), calls=%async_computation.21 | async-start | bytes 8388608
  1281.6 39.6 %slice-start.5 = ((s8[9437184]{0:T(1024)(128)(4,1)}), s8[1048576]{0:T(1024)(128)(4,1)S(1)}, s32[]{:S(2)}) async-start(s8[9437184]{0:T(1024)(128)(4,1)} %bitcast.308), calls=%async_computation.19 | async-start | bytes 2097152
  1281.6 39.6 %slice-start.8 = ((s8[9437184]{0:T(1024)(128)(4,1)}), s8[1048576]{0:T(1024)(128)(4,1)S(1)}, s32[]{:S(2)}) async-start(s8[9437184]{0:T(1024)(128)(4,1)} %bitcast.310), calls=%async_computation.22 | async-start | bytes 2097152
  1451.4 46.1 %slice-start = ((s8[9437184]{0:T(1024)(128)(4,1)}), s8[1048576]{0:T(1024)(128)(4,1)S(1)}, s32[]{:S(2)}) async-start(s8[9437184]{0:T(1024)(128)(4,1)} %bitcast.306), calls=%async_computation.14 | async-start | bytes 2097152
  1470.2 27.4 %slice-start.1 = ((s8[9437184]{0:T(1024)(128)(4,1)}), s8[4194304]{0:T(1024)(128)(4,1)S(1)}, s32[]{:S(2)}) async-start(s8[9437184]{0:T(1024)(128)(4,1)} %bitcast.306), calls=%async_computation.15 | async-start | bytes 8388608
  1470.2 27.4 %slice-start.2 = ((s8[9437184]{0:T(1024)(128)(4,1)}), s8[4194304]{0:T(1024)(128)(4,1)S(1)}, s32[]{:S(2)}) async-start(s8[9437184]{0:T(1024)(128)(4,1)} %bitcast.306), calls=%async_computation.16 | async-start | bytes 8388608
  1678.5 70.5 %copy-start.1 = (bf16[2048,768]{0,1:T(8,128)(2,1)S(1)}, bf16[2048,768]{0,1:T(8,128)(2,1)}, u32[]{:S(2)}) copy-start(bf16[2048,768]{0,1:T(8,128)(2,1)} %copy.32) | copy-start | bytes 9437188
Sparse Core Ops, SparseCore 0:
  472.8 48.3 all-gather.9
  562.0 46.1 all-gather.11
  650.3 46.1 all-gather.13
  738.4 46.4 all-gather.15
  826.5 43.3 all-gather.17
  920.5 61.5 all-gather.19
  1052.6 61.7 all-gather.7
where the time goes:
time: 1790 us; the launch traced here: 1780 us
  matrix products  816 us (46%)
  other arithmetic  425 us (24%)
  blocking collectives  334 us (19%)
  local copies, waits for them, and re-layouts  135 us (8%)
  waiting for transfers between devices  38.7 us (2%)
  between operations  24.3 us (1%)
    all_to_all x5, blocking collectives, group_sum(): lax.all_to_all(g, 'data', 0, 0, tiled=True).reshape(p, rows // p, cols)  334 us
    dot_general x3, matrix products, forward(): jnp.dot(h.astype(BF), w1b[l], preferred_element_type=F32)  210 us
    dot_general x3, matrix products, step(): a = jnp.dot(h.astype(BF), w1b[l], preferred_element_type=F32)  202 us
    reduce_sum x6, other arithmetic, lamb(): r = jnp.sqrt(jnp.sum(w * w)) / jnp.sqrt(jnp.sum(u * u))  193 us
    another operation x6, other arithmetic, stacked(): return jnp.stack([u[k] for u in ups])  172 us
    unnamed x46, local copies, waits for them, and re-layouts  127 us
    dot_general x3, matrix products, step(): jnp.dot(gb, w2b[l].T, preferred_element_type=F32) * gelu_grad(a)  74.1 us
    dot_general x3, matrix products, forward(): h = h + jnp.dot(s, w2b[l], preferred_element_type=F32)  61.9 us
  transfers between devices with their start and end apart: 9, of which 2 were waited for; matrix products, arithmetic and copies ran while one was open for 31% of the time, Pallas kernels for 0%

commit v1 on v0

v1 whole, which is shorter than its diff:
```python
import functools

import jax
import jax.numpy as jnp
from jax import lax
from jax.experimental import pallas as pl
from jax.experimental.pallas import tpu as pltpu
from jax.sharding import PartitionSpec as P

BETA1 = 0.9
BETA2 = 0.999
BC1 = 1.0 / (1.0 - BETA1 ** 10)
BC2 = 1.0 / (1.0 - BETA2 ** 10)
EPS = 1e-12
WD = 0.01
ETA = 0.05
R2 = 0.7071067811865476
R2PI = 0.3989422804014327
BF = jnp.bfloat16
F32 = jnp.float32
VMEM = 67043328
ANY = pl.BlockSpec(memory_space=pl.ANY)

D2D = [(0, 1), (1, 0), (2, 3), (3, 2)]
CROSS = [(0, 2), (2, 0), (1, 3), (3, 1)]
DIAG = [(0, 3), (3, 0), (1, 2), (2, 1)]


def dot(a, b):
    return jnp.dot(a, b, preferred_element_type=F32)


def dot_nt(a, b):
    return lax.dot_general(a, b, (((1,), (1,)), ((), ())), preferred_element_type=F32)


def dot_tn(a, b):
    return lax.dot_general(a, b, (((0,), (0,)), ((), ())), preferred_element_type=F32)


def gelu(a):
    return (0.5 * a) * (1.0 + lax.erf(a * R2))


def gelu_grad(a):
    return 0.5 * (1.0 + lax.erf(a * R2)) + a * jnp.exp(-0.5 * a * a) * R2PI


def params(*sem):
    return pltpu.CompilerParams(vmem_limit_bytes=VMEM, dimension_semantics=sem)


def cost(flops, nbytes):
    return pl.CostEstimate(flops=int(flops), bytes_accessed=int(nbytes), transcendentals=0)


def in_kernel(x_ref, w_ref, o_ref):
    @pl.when(pl.program_id(0) == 0)
    def _():
        o_ref[...] = jnp.zeros_like(o_ref)

    o_ref[...] += dot(x_ref[...], w_ref[...].astype(BF))


def in_matmul(x, w, kb=768):
    t, e = x.shape
    d = w.shape[1]
    return pl.pallas_call(
        in_kernel,
        grid=(e // kb,),
        in_specs=[pl.BlockSpec((t, kb), lambda k: (0, k)), pl.BlockSpec((kb, d), lambda k: (k, 0))],
        out_specs=pl.BlockSpec((t, d), lambda k: (0, 0)),
        out_shape=jax.ShapeDtypeStruct((t, d), F32),
        compiler_params=params("arbitrary"),
        cost_estimate=cost(2 * t * e * d, 2 * t * e + w.nbytes + 4 * t * d),
        name="in_matmul",
    )(x, w)


def chain_kernel(scale, dev, nm, c_ref, h_ref, y_ref, w1_hbm, w2_hbm, *rest):
    hb_o, s_o, gb_o, e_o, g0_o, w1, w2, a_s, s_s, h_s, sem = rest[4 * (dev > 0):]
    t = pl.program_id(0)
    c = c_ref[0]
    nl, _, f = w1.shape
    half = f // 2
    fc = half // nm

    def copies(l):
        out = []
        for k in range(2):
            src = pl.multiple_of(lax.rem(c + k, 2) * half, half)
            out.append(pltpu.make_async_copy(w1_hbm.at[l, :, pl.ds(src, half)], w1.at[l, :, pl.ds(k * half, half)],
                                             sem.at[l, k]))
            out.append(pltpu.make_async_copy(w2_hbm.at[l, pl.ds(src, half), :], w2.at[l, pl.ds(k * half, half), :],
                                             sem.at[l, k + 2]))
        return out

    @pl.when(t == 0)
    def _():
        for l in range(nl):
            for cp in copies(l):
                cp.start()

    h_s[...] = h_ref[...]

    def piece(o, l, j):
        return o.at[0, l, :, j * fc:(j + 1) * fc] if j < nm else s_s.at[:, (j - nm) * fc:(j - nm + 1) * fc]

    def fwd(l, carry):
        @pl.when(t == 0)
        def _():
            for cp in copies(l):
                cp.wait()

        hb_o[0, l] = h_s[...].astype(BF)

        def up(j):
            a_s[l, :, j * fc:(j + 1) * fc] = dot(hb_o[0, l], w1[l, :, j * fc:(j + 1) * fc])

        up(0)
        for j in range(2 * nm):
            if j + 1 < 2 * nm:
                up(j + 1)
            piece(s_o, l, j)[...] = gelu(a_s[l, :, j * fc:(j + 1) * fc]).astype(BF)
            h_s[...] += dot(piece(s_o, l, j)[...], w2[l, j * fc:(j + 1) * fc, :])
        return carry

    def bwd(k, carry):
        l = nl - 1 - k
        gb_o[0, l] = h_s[...].astype(BF)

        def down(j):
            return dot_nt(gb_o[0, l], w2[l, j * fc:(j + 1) * fc, :])

        de = down(0)
        for j in range(2 * nm):
            nxt = down(j + 1) if j + 1 < 2 * nm else None
            piece(e_o, l, j)[...] = (de * gelu_grad(a_s[l, :, j * fc:(j + 1) * fc])).astype(BF)
            h_s[...] += dot_nt(piece(e_o, l, j)[...], w1[l, :, j * fc:(j + 1) * fc])
            de = nxt
        return carry

    lax.fori_loop(0, nl, fwd, 0)
    h_s[...] = (h_s[...] - y_ref[...].astype(F32)) * scale
    lax.fori_loop(0, nl, bwd, 0)
    g0_o[...] = h_s[...].astype(BF)


def chain(c, h, y, w1, w2, scale, prev=None, tm=256, nm=2):
    t, d = h.shape
    nl, _, f = w1.shape
    half = f // 2
    dev = 0 if prev is None else 1
    tok = pl.BlockSpec((tm, d), lambda i, c: (i, 0))

    def out(w):
        return pl.BlockSpec((1, nl, tm, w), lambda i, c: (dev, 0, i, 0))

    shapes = [jax.ShapeDtypeStruct((2, nl, t, w), BF) for w in (d, half, d, half)]
    return pl.pallas_call(
        functools.partial(chain_kernel, scale, dev, nm),
        grid_spec=pltpu.PrefetchScalarGridSpec(
            num_scalar_prefetch=1,
            grid=(t // tm,),
            in_specs=[tok, tok, ANY, ANY] + [ANY] * (4 * dev),
            out_specs=[out(d), out(half), out(d), out(half), tok],
            scratch_shapes=[
                pltpu.VMEM((nl, d, f), BF),
                pltpu.VMEM((nl, f, d), BF),
                pltpu.VMEM((nl, tm, f), F32),
                pltpu.VMEM((tm, half), BF),
                pltpu.VMEM((tm, d), F32),
                pltpu.SemaphoreType.DMA((nl, 4)),
            ],
        ),
        out_shape=shapes + [jax.ShapeDtypeStruct((t, d), BF)],
        input_output_aliases={5 + k: k for k in range(4 * dev)},
        compiler_params=params("arbitrary"),
        cost_estimate=cost(8 * nl * t * d * f, 4 * nl * d * f + 8 * t * d + 4 * nl * t * (d + half)),
        name="chain_%d" % dev,
    )(c, h, y, w1, w2, *(prev or ()))


def dw_kernel(i_ref, hb_ref, s_ref, gb_ref, e_ref, sp_o, sm_o, acc):
    job, dev, k = pl.program_id(0), pl.program_id(1), pl.program_id(2)
    nk = pl.num_programs(2)

    def product(a_ref, b_ref):
        acc[...] = jnp.where(k == 0, 0.0, acc[...]) + dot_tn(a_ref[0, 0], b_ref[0, 0])

    @pl.when(job % 2 == 0)
    def _():
        product(s_ref, gb_ref)

    @pl.when(job % 2 == 1)
    def _():
        product(hb_ref, e_ref)

    def add(o):
        r = acc[...].astype(BF).astype(F32)
        o[0] = jnp.where(dev == 0, 0.0, o[0]) + r

    @pl.when((k == nk - 1) & (job < 2))
    def _():
        add(sp_o)

    @pl.when((k == nk - 1) & (job >= 2))
    def _():
        add(sm_o)


def dw_half(core, acts, l, kb=1024):
    hb, s, gb, e = acts
    t, d = hb.shape[2:]
    q = s.shape[3] // 2

    def quarter(job, core):
        return jnp.where(job < 2, 1 - core, core)

    def feat(odd):
        def index(job, dev, k, c):
            mine = job % 2 == odd
            return (jnp.where(mine, dev, 0), l, jnp.where(mine, k, 0), quarter(job, c[0]))
        return index

    def full(odd):
        def index(job, dev, k, c):
            mine = job % 2 == odd
            return (jnp.where(mine, dev, 0), l, jnp.where(mine, k, 0), 0)
        return index

    blk = (1, 1, kb, q)
    return pl.pallas_call(
        dw_kernel,
        grid_spec=pltpu.PrefetchScalarGridSpec(
            num_scalar_prefetch=1,
            grid=(4, 2, t // kb),
            in_specs=[pl.BlockSpec((1, 1, kb, d), full(1)), pl.BlockSpec(blk, feat(0)),
                      pl.BlockSpec((1, 1, kb, d), full(0)), pl.BlockSpec(blk, feat(1))],
            out_specs=[pl.BlockSpec((1, d, d), lambda job, dev, k, c: (jnp.minimum(job, 1), 0, 0)),
                       pl.BlockSpec((1, d, d), lambda job, dev, k, c: (jnp.maximum(job - 2, 0), 0, 0))],
            scratch_shapes=[pltpu.VMEM((d, d), F32)],
        ),
        out_shape=[jax.ShapeDtypeStruct((2, d, d), F32)] * 2,
        compiler_params=params("arbitrary", "arbitrary", "arbitrary"),
        cost_estimate=cost(16 * t * d * d, 16 * t * d * 2 + 16 * d * d),
        name="dw_%d" % l,
    )(core, hb, s, gb, e)


def dwi_kernel(q_ref, x_ref, g_ref, o_ref):
    o_ref[...] = dot_tn(x_ref[...], g_ref[...]).astype(BF)


def dwi_quarter(q, x, g, mb=512):
    t, e = x.shape
    d = g.shape[1]
    n = e // 4 // mb
    return pl.pallas_call(
        dwi_kernel,
        grid_spec=pltpu.PrefetchScalarGridSpec(
            num_scalar_prefetch=1,
            grid=(n,),
            in_specs=[pl.BlockSpec((t, mb), lambda j, q: (0, q[0] * n + j)), pl.BlockSpec((t, d), lambda j, q: (0, 0))],
            out_specs=pl.BlockSpec((mb, d), lambda j, q: (j, 0)),
        ),
        out_shape=jax.ShapeDtypeStruct((e // 4, d), BF),
        compiler_params=params("arbitrary"),
        cost_estimate=cost(2 * t * e * d // 4, t * e // 2 + 2 * t * d),
        name="dwi",
    )(q, x, g)


def lamb_kernel(nb, gi, i_ref, *refs):
    w_ref, m_ref, v_ref, g0, g1, g2, g3 = refs[:7]
    wn_o, mn_o, vn_o, wb_o, w_s, u_s, sw, su, ratio = refs[-9:]
    p, k, j = pl.program_id(0), pl.program_id(1), pl.program_id(2)
    slot = k * nb + j
    shape = w_s.shape[1:]
    first = (k == 0) & (j == 0)

    @pl.when((p == 0) & first)
    def _():
        sw[...] = jnp.zeros_like(sw)
        su[...] = jnp.zeros_like(su)

    def sweep(g_ref):
        w = w_ref[...].reshape(shape)
        g = g_ref[...].reshape(shape).astype(F32)
        m2 = BETA1 * m_ref[...].reshape(shape) + (1.0 - BETA1) * g
        v2 = BETA2 * v_ref[...].reshape(shape) + (1.0 - BETA2) * g * g
        u = BC1 * m2 / (jnp.sqrt(BC2 * v2) + EPS) + WD * w
        mn_o[...] = m2.reshape(mn_o.shape)
        vn_o[...] = v2.reshape(vn_o.shape)
        w_s[slot] = w
        u_s[slot] = u
        sw[...] += jnp.sum((w * w).reshape(-1, 8, shape[1]), axis=0)
        su[...] += jnp.sum((u * u).reshape(-1, 8, shape[1]), axis=0)

    for kk, g_ref in enumerate((g0, g1, g2, g3)):
        @pl.when((p == 0) & (k == kk))
        def _(g_ref=g_ref):
            sweep(g_ref)

    @pl.when((p == 1) & first)
    def _():
        ratio[0] = ETA * (jnp.sqrt(jnp.sum(sw[...])) / jnp.sqrt(jnp.sum(su[...])))

    @pl.when(p == 1)
    def _():
        w = w_s[slot] - ratio[0] * u_s[slot]
        wn_o[...] = w.reshape(wn_o.shape)
        wb_o[...] = w.astype(BF)


def lamb(i, w, m, v, gs, gi, l, bufs, cols, rb):
    rows, width = w.shape[-2:]
    gr, gw = gs[0].shape[-2:]
    nb = gr // rb
    lead = () if l is None else (l,)
    one = () if l is None else (1,)

    def where(p, k, j, i):
        q = jnp.bitwise_xor(k, i[0])
        return (j, q) if cols else (q * nb + j, 0)

    def at_first(p, k, j, i):
        k, j = jnp.where(p == 0, k, 3), jnp.where(p == 0, j, nb - 1)
        return lead + where(p, k, j, i)

    def at_second(p, k, j, i):
        k, j = jnp.where(p == 1, k, 0), jnp.where(p == 1, j, 0)
        return lead + where(p, k, j, i)

    def at_second2(p, k, j, i):
        k, j = jnp.where(p == 1, k, 0), jnp.where(p == 1, j, 0)
        return where(p, k, j, i)

    def at_g(kk):
        def index(p, k, j, i):
            b = jnp.where((p == 1) | (k > kk), nb - 1, jnp.where(k < kk, 0, j))
            return (b, 0) if gi is None else (gi, b, 0)
        return index

    blk = one + (rb, gw)
    gblk = (rb, gw) if gi is None else (1, rb, gw)
    n = len(bufs)
    f32 = jax.ShapeDtypeStruct(w.shape, F32)
    return pl.pallas_call(
        functools.partial(lamb_kernel, nb, gi),
        grid_spec=pltpu.PrefetchScalarGridSpec(
            num_scalar_prefetch=1,
            grid=(2, 4, nb),
            in_specs=[pl.BlockSpec(blk, at_first)] * 3 + [pl.BlockSpec(gblk, at_g(kk)) for kk in range(4)] + [ANY] * n,
            out_specs=[pl.BlockSpec(blk, at_second), pl.BlockSpec(blk, at_first), pl.BlockSpec(blk, at_first),
                       pl.BlockSpec((rb, gw), at_second2)],
            scratch_shapes=[
                pltpu.VMEM((4 * nb, rb, gw), F32),
                pltpu.VMEM((4 * nb, rb, gw), F32),
                pltpu.VMEM((8, gw), F32),
                pltpu.VMEM((8, gw), F32),
                pltpu.SMEM((1,), F32),
            ],
        ),
        out_shape=[f32, f32, f32, jax.ShapeDtypeStruct((rows, width), BF)],
        input_output_aliases={8 + k: k for k in range(n)},
        compiler_params=params("arbitrary", "arbitrary", "arbitrary"),
        cost_estimate=cost(30 * rows * width * 30, 28 * rows * width),
        name="lamb",
    )(i, w, m, v, *gs, *bufs)


def fwd_kernel(nl, nj, h_ref, *refs):
    w1_hbm, w2_hbm = refs[:nl], refs[nl:2 * nl]
    o_ref, w1, w2, a_s, s_s, sem = refs[2 * nl:]
    t = pl.program_id(0)
    fc = w1.shape[2] // nj

    @pl.when(t == 0)
    def _():
        for l in range(nl):
            pltpu.make_async_copy(w1_hbm[l], w1.at[l], sem.at[l, 0]).start()
            pltpu.make_async_copy(w2_hbm[l], w2.at[l], sem.at[l, 1]).start()

    o_ref[...] = h_ref[...]

    def layer(l, carry):
        @pl.when(t == 0)
        def _():
            pltpu.make_async_copy(w1_hbm[0], w1.at[l], sem.at[l, 0]).wait()
            pltpu.make_async_copy(w2_hbm[0], w2.at[l], sem.at[l, 1]).wait()

        hb = o_ref[...].astype(BF)

        def up(j):
            a_s[:, j * fc:(j + 1) * fc] = dot(hb, w1[l, :, j * fc:(j + 1) * fc])

        up(0)
        for j in range(nj):
            if j + 1 < nj:
                up(j + 1)
            s_s[:, j * fc:(j + 1) * fc] = gelu(a_s[:, j * fc:(j + 1) * fc]).astype(BF)
            o_ref[...] += dot(s_s[:, j * fc:(j + 1) * fc], w2[l, j * fc:(j + 1) * fc, :])
        return carry

    lax.fori_loop(0, nl, layer, 0)


def forward(h, w1, w2, tm=256, nj=4):
    t, d = h.shape
    nl = len(w1)
    f = w1[0].shape[1]
    tok = pl.BlockSpec((tm, d), lambda i: (i, 0))
    return pl.pallas_call(
        functools.partial(fwd_kernel, nl, nj),
        grid=(t // tm,),
        in_specs=[tok] + [ANY] * (2 * nl),
        out_specs=tok,
        out_shape=jax.ShapeDtypeStruct((t, d), F32),
        scratch_shapes=[
            pltpu.VMEM((nl, d, f), BF),
            pltpu.VMEM((nl, f, d), BF),
            pltpu.VMEM((tm, f), F32),
            pltpu.VMEM((tm, f), BF),
            pltpu.SemaphoreType.DMA((nl, 2)),
        ],
        compiler_params=params("arbitrary"),
        cost_estimate=cost(4 * nl * t * d * f, 4 * nl * d * f + 8 * t * d),
        name="forward",
    )(h, *w1, *w2)


def solution(mesh):
    p = mesh.shape['data']

    def step(wi, w1, w2, mi, vi, m1, v1, m2, v2, x0, y0, x1, y1):
        nl, d, f = w1.shape
        scale = 1.0 / (x0.shape[0] * p * d)
        i = lax.axis_index('data').astype(jnp.int32)
        me = jnp.reshape(i, (1,))
        chip = me // 2
        core = me % 2

        def send(x, perm):
            return lax.ppermute(x, 'data', perm)

        def gather(g):
            far = send(g, CROSS)
            return g, send(g, D2D), far, send(far, D2D)

        w1b, w2b = w1.astype(BF), w2.astype(BF)
        y0o = send(y0, CROSS)
        h0 = in_matmul(x0, wi)
        h0o = send(h0, CROSS)
        *acts, g0 = chain(chip, h0, y0, w1b, w2b, scale)
        pieces = {k: dwi_quarter(jnp.bitwise_xor(me, k), x0, g0) for k in (2, 3, 1, 0)}
        got = [pieces[0], send(pieces[1], D2D), send(pieces[2], CROSS), send(pieces[3], DIAG)]
        si = sum(g.astype(F32) for g in got).astype(BF)
        gi = gather(si)
        *acts, _ = chain(chip, h0o, y0o, w1b, w2b, scale, acts)
        gl = []
        for l in range(nl):
            sp, sm = dw_half(core, acts, l)
            gl.append(gather((sm + send(sp, D2D)).astype(BF)))
        wi_n, mi_n, vi_n, wib = lamb(me, wi, mi, vi, gi, None, None, (), False, 384)
        b1, b2 = (), ()
        w1n, w2n = [], []
        for l in range(nl):
            *b1, wb = lamb(me, w1, m1, v1, gl[l], 1, l, b1, True, 384)
            w1n.append(wb)
            *b2, wb = lamb(me, w2, m2, v2, gl[l], 0, l, b2, False, 384)
            w2n.append(wb)
        h1 = forward(in_matmul(x1, wib), w1n, w2n)
        loss = jnp.sum((h1 - y1.astype(F32)) ** 2, axis=-1) / (2.0 * d)
        return (wi_n, b1[0], b2[0], mi_n, vi_n, b1[1], b1[2], b2[1], b2[2], loss, h1)

    w2s = P('rep', None)
    w3s = P('rep', None, None)
    ts = P(('rep', 'data'), None)
    return jax.shard_map(step, mesh=mesh,
                         in_specs=(w2s, w3s, w3s, w2s, w2s, w3s, w3s, w3s, w3s, ts, ts, ts, ts),
                         out_specs=(w2s, w3s, w3s, w2s, w2s, w3s, w3s, w3s, w3s, P(('rep', 'data')), ts),
                         check_vma=False)
```

time: 1790 us -> 997 us (0.56)
  matrix products: 816 us -> 0 us
  Pallas kernels: 0 us -> 773 us
  other arithmetic: 425 us -> 46.6 us
  blocking collectives: 334 us -> 0 us
  local copies, waits for them, and re-layouts: 135 us -> 6.99 us
  waiting for transfers between devices: 38.7 us -> 147 us
  between operations: 24.3 us -> 1.38 us
    dot_general x27 -> x0, matrix products: 816 us -> none  [the longest x3 210 us: forward(): jnp.dot(h.astype(BF), w1b[l], preferred_element_type=F32)]
    pallas_call x0 -> x19, Pallas kernels: none -> 773 us  [the longest x2 282 us: chain(): pl.pallas_call(functools.partial(chain_kernel, scale, dev, nm), grid_spec...]
    all_to_all x5 -> x0, blocking collectives: 334 us -> none  [group_sum(): lax.all_to_all(g, 'data', 0, 0, tiled=True).reshape(p, rows // p, cols)]
    reduce_sum x13 -> x1, other arithmetic: 227 us -> 4.64 us  [step(): loss = jnp.sum((h1 - y1.astype(F32)) ** 2, axis=-1) / (2.0 * d)]
    another operation x6 -> x0, other arithmetic: 172 us -> none  [stacked(): return jnp.stack([u[k] for u in ups])]
    ppermute x0 -> x20, waiting for transfers between devices: none -> 147 us  [send(): return lax.ppermute(x, 'data', perm)]
    unnamed x46 -> x20, local copies, waits for them, and re-layouts: 127 us -> 6.99 us
    convert_element_type x0 -> x6, other arithmetic: none -> 41.4 us  [the longest x2 22.2 us: step(): w1b, w2b = (w1.astype(BF), w2.astype(BF))]
  transfers between devices with their start and end apart: 9 -> 20, of which waited for: 2 -> 4; matrix products, arithmetic and copies ran while one was open for 31% -> 4% of each run, Pallas kernels for 0% -> 63%
where the time goes in v1:
time: 997 us; the launch traced here: 989 us
  Pallas kernels  773 us (78%)
  waiting for transfers between devices  147 us (15%)
  other arithmetic  46.6 us (5%)
  starting transfers between devices  13 us (1%)
    pallas_call x2, Pallas kernels, chain(): pl.pallas_call(functools.partial(chain_kernel, scale, dev, nm), grid_spec...  282 us
    pallas_call x7, Pallas kernels, lamb(): pl.pallas_call(functools.partial(lamb_kernel, nb, gi), grid_spec=pltpu.Pr...  224 us
    ppermute x20, waiting for transfers between devices, send(): return lax.ppermute(x, 'data', perm)  147 us
    pallas_call x3, Pallas kernels, dw_half(): pl.pallas_call(dw_kernel, grid_spec=pltpu.PrefetchScalarGridSpec(num_scal...  108 us
    pallas_call x1, Pallas kernels, forward(): pl.pallas_call(functools.partial(fwd_kernel, nl, nj), grid=(t // tm,), in...  69.4 us
    pallas_call x2, Pallas kernels, in_matmul(): pl.pallas_call(in_kernel, grid=(e // kb,), in_specs=[pl.BlockSpec((t, kb)...  53.4 us
    pallas_call x4, Pallas kernels, dwi_quarter(): pl.pallas_call(dwi_kernel, grid_spec=pltpu.PrefetchScalarGridSpec(num_sca...  36.2 us
    convert_element_type x2, other arithmetic, step(): w1b, w2b = (w1.astype(BF), w2.astype(BF))  22.2 us
  transfers between devices with their start and end apart: 20, of which 4 were waited for; matrix products, arithmetic and copies ran while one was open for 4% of the time, Pallas kernels for 63%

profile of v1, /device:TPU:0, one launch (start us, length us, event | category | flops | bytes accessed | tf_op | source)
XLA Modules:
  0.0 988.6 jit_solution(10407947630885046762)
XLA Ops:
  0.6 26.9 %in_matmul.2.h_ref = f32[2048,768]{1,0:T(8,128)} custom-call(bf16[2048,6144]{1,0:T(8,128)(2,1)} %x_ref.10, f32[6144,768]{1,0:T(8,128)} %refs_0_.7), custom_call_target="tpu_custom_call" | custom-call | flops 19327352832 | bytes 50331648 | tf_op jit(solution)/shard_map/in_matmul/pallas_call | solution.py:68
  27.6 3.3 collective-permute-start.6
  30.9 0.0 collective-permute-start.7
  30.9 16.2 %convert_element_type.33.w1_hbm = bf16[3,768,3072]{2,1,0:T(8,128)(2,1)} convert(f32[3,768,3072]{2,1,0:T(8,128)} %refs_0_.10) | non-fusion elementwise | flops 7077888 | bytes 42467328 | tf_op jit(solution)/shard_map/convert_element_type | solution.py:451
  47.2 6.1 copy-done
  53.2 6.0 convert_element_type.34.w2_hbm
  59.2 141.1 %chain_0.1 = (bf16[2,3,2048,768]{3,2,1,0:T(8,128)(2,1)}, bf16[2,3,2048,1536]{3,2,1,0:T(8,128)(2,1)}, bf16[2,3,2048,768]{3,2,1,0:T(8,128)(2,1)}, bf16[2,3,2048,1536]{3,2,1,0:T(8,128)(2,1)}, bf16[2048,768]{1,0:T(8,128)(2,1)}) custom-call(s32[1]{0:T(128)S(6)} %select_n.12.c_ref, f32[2048,768]{1,0:T(8,128)} %in_matmul.2.h_ref, bf16[2048,768]{1,0:T(8,128)(2,1)} %y_ref.1, ...), custom_call_target="tpu_custom_call" | custom-call | flops 115964116992 | bytes 97517568 | tf_op jit(solution)/shard_map/chain_0/pallas_call | solution.py:160
  200.3 9.1 dwi.5
  209.4 9.0 dwi.6
  218.4 2.0 collective-permute-start.1
  220.4 9.2 dwi.7
  229.5 0.1 collective-permute-start.2
  229.7 5.0 collective-permute-done.7.y_ref
  234.7 141.0 %chain_1.1 = (bf16[2,3,2048,768]{3,2,1,0:T(8,128)(2,1)}, bf16[2,3,2048,1536]{3,2,1,0:T(8,128)(2,1)}, bf16[2,3,2048,768]{3,2,1,0:T(8,128)(2,1)}, bf16[2,3,2048,1536]{3,2,1,0:T(8,128)(2,1)}, bf16[2048,768]{1,0:T(8,128)(2,1)}) custom-call(s32[1]{0:T(128)S(6)} %select_n.12.c_ref, ...), custom_call_target="tpu_custom_call", output_to_operand_aliasing={{0}: (5, {}), {1}: (6, {}), {2}: (7, {}), {3}: (8, {})} | custom-call | flops 115964116992 | bytes 97517568 | tf_op jit(solution)/shard_map/chain_1/pallas_call | solution.py:160
  375.7 36.1 %dw_0.1 = (f32[2,768,768]{2,1,0:T(8,128)}, f32[2,768,768]{2,1,0:T(8,128)}) custom-call(s32[1]{0:T(128)S(6)} %select_n.13.i_ref, bf16[2,3,2048,768]{3,2,1,0:T(8,128)(2,1)} %get-tuple-element.60.hb_ref, bf16[2,3,2048,1536]{3,2,1,0:T(8,128)(2,1)} %get-tuple-element.61.s_ref, bf16[2,3,2048,768]{3,2,1,0:T(8,128)(2,1)} %get-tuple-element.62.gb_ref, ...), custom_call_target="tpu_custom_call" | custom-call | flops 19327352832 | bytes 59768832 | tf_op jit(solution)/shard_map/dw_0/pallas_call | solution.py:233
  411.7 36.3 %dw_1.1 = (f32[2,768,768]{2,1,0:T(8,128)}, f32[2,768,768]{2,1,0:T(8,128)}) custom-call(s32[1]{0:T(128)S(6)} %select_n.13.i_ref, bf16[2,3,2048,768]{3,2,1,0:T(8,128)(2,1)} %get-tuple-element.60.hb_ref, bf16[2,3,2048,1536]{3,2,1,0:T(8,128)(2,1)} %get-tuple-element.61.s_ref, bf16[2,3,2048,768]{3,2,1,0:T(8,128)(2,1)} %get-tuple-element.62.gb_ref, ...), custom_call_target="tpu_custom_call" | custom-call | flops 19327352832 | bytes 59768832 | tf_op jit(solution)/shard_map/dw_1/pallas_call | solution.py:233
  448.0 0.5 collective-permute-start.12
  448.5 36.0 %dw_2.1 = (f32[2,768,768]{2,1,0:T(8,128)}, f32[2,768,768]{2,1,0:T(8,128)}) custom-call(s32[1]{0:T(128)S(6)} %select_n.13.i_ref, bf16[2,3,2048,768]{3,2,1,0:T(8,128)(2,1)} %get-tuple-element.60.hb_ref, bf16[2,3,2048,1536]{3,2,1,0:T(8,128)(2,1)} %get-tuple-element.61.s_ref, bf16[2,3,2048,768]{3,2,1,0:T(8,128)(2,1)} %get-tuple-element.62.gb_ref, ...), custom_call_target="tpu_custom_call" | custom-call | flops 19327352832 | bytes 59768832 | tf_op jit(solution)/shard_map/dw_2/pallas_call | solution.py:233
  484.5 0.1 collective-permute-start.8
  484.6 9.0 dwi.4
  493.6 5.1 add_convert_fusion.3.refs_3_
  498.7 1.9 collective-permute-start.4
  500.6 0.2 collective-permute-start.3
  500.7 51.7 %collective-permute-done.4.refs_5_ = bf16[1536,768]{1,0:T(8,128)(2,1)S(1)} collective-permute-done((bf16[1536,768]{1,0:T(8,128)(2,1)S(1)}, bf16[1536,768]{1,0:T(8,128)(2,1)S(1)}, u32[]{:S(2)}, u32[]{:S(2)}) %collective-permute-start.4) | collective-permute-done | bytes 2359328 | tf_op jit(solution)/shard_map/ppermute | solution.py:445
  552.5 0.0 slice-start.3
  552.5 5.3 add_convert_fusion.refs_3_
  557.7 1.7 collective-permute-start.18
  559.5 4.5 add_convert_fusion.1.refs_3_
  564.0 0.3 collective-permute-start.14
  564.3 4.4 add_convert_fusion.2.refs_3_
  568.7 1.7 collective-permute-start.10
  570.5 41.4 %collective-permute-done.18.refs_5_ = bf16[2,768,768]{2,1,0:T(8,128)(2,1)} collective-permute-done((bf16[2,768,768]{2,1,0:T(8,128)(2,1)}, bf16[2,768,768]{2,1,0:T(8,128)(2,1)}, u32[]{:S(2)}, u32[]{:S(2)}) %collective-permute-start.18) | collective-permute-done | bytes 2359328 | tf_op jit(solution)/shard_map/ppermute | solution.py:445
  611.9 0.5 collective-permute-start.13
  612.4 0.9 copy-done.5
  613.3 49.1 %collective-permute-done.14.refs_5_ = bf16[2,768,768]{2,1,0:T(8,128)(2,1)} collective-permute-done((bf16[2,768,768]{2,1,0:T(8,128)(2,1)}, bf16[2,768,768]{2,1,0:T(8,128)(2,1)}, u32[]{:S(2)}, u32[]{:S(2)}) %collective-permute-start.14) | collective-permute-done | bytes 2359328 | tf_op jit(solution)/shard_map/ppermute | solution.py:445
  662.4 54.4 %lamb.7 = (f32[6144,768]{1,0:T(8,128)}, f32[6144,768]{1,0:T(8,128)}, f32[6144,768]{1,0:T(8,128)}, bf16[6144,768]{1,0:T(8,128)(2,1)}) custom-call(s32[1]{0:T(128)} %bitcast.q_ref.i_ref, f32[6144,768]{1,0:T(8,128)} %refs_0_.7, f32[6144,768]{1,0:T(8,128)} %refs_1_.7, f32[6144,768]{1,0:T(8,128)} %refs_2_.7, bf16[1536,768]{1,0:T(8,128)(2,1)} %copy-done.1, ...), custom_call_target="tpu_custom_call" | custom-call | flops 4246732800 | bytes 132120576 | tf_op jit(solution)/shard_map/lamb/pallas_call | solution.py:349
  716.8 0.5 collective-permute-start.9
  717.3 0.0 collective-permute-start.11
  717.4 26.4 %in_matmul.3.h_ref = f32[2048,768]{1,0:T(8,128)} custom-call(bf16[2048,6144]{1,0:T(8,128)(2,1)} %x_ref.11, bf16[6144,768]{1,0:T(8,128)(2,1)} %get-tuple-element.90.w_ref), custom_call_target="tpu_custom_call" | custom-call | flops 19327352832 | bytes 40894464 | tf_op jit(solution)/shard_map/in_matmul/pallas_call | solution.py:68
  743.8 28.3 %lamb.11 = (f32[3,3072,768]{2,1,0:T(8,128)}, f32[3,3072,768]{2,1,0:T(8,128)}, f32[3,3072,768]{2,1,0:T(8,128)}, bf16[3072,768]{1,0:T(8,128)(2,1)}) custom-call(s32[1]{0:T(128)} %bitcast.q_ref.i_ref, f32[3,3072,768]{2,1,0:T(8,128)} %refs_0_.13, f32[3,3072,768]{2,1,0:T(8,128)} %refs_1_.13, f32[3,3072,768]{2,1,0:T(8,128)} %refs_2_.13, ...), custom_call_target="tpu_custom_call" | custom-call | flops 2123366400 | bytes 66060288 | tf_op jit(solution)/shard_map/lamb/pallas_call | solution.py:349
  772.1 28.4 %lamb.8 = (f32[3,768,3072]{2,1,0:T(8,128)}, f32[3,768,3072]{2,1,0:T(8,128)}, f32[3,768,3072]{2,1,0:T(8,128)}, bf16[768,3072]{1,0:T(8,128)(2,1)}) custom-call(s32[1]{0:T(128)} %bitcast.q_ref.i_ref, f32[3,768,3072]{2,1,0:T(8,128)} %refs_0_.10, f32[3,768,3072]{2,1,0:T(8,128)} %refs_1_.10, f32[3,768,3072]{2,1,0:T(8,128)} %refs_2_.10, ...), custom_call_target="tpu_custom_call" | custom-call | flops 2123366400 | bytes 66060288 | tf_op jit(solution)/shard_map/lamb/pallas_call | solution.py:349
  800.5 28.1 %lamb.12 = (f32[3,3072,768]{2,1,0:T(8,128)}, f32[3,3072,768]{2,1,0:T(8,128)}, f32[3,3072,768]{2,1,0:T(8,128)}, bf16[3072,768]{1,0:T(8,128)(2,1)}) custom-call(s32[1]{0:T(128)} %bitcast.q_ref.i_ref, f32[3,3072,768]{2,1,0:T(8,128)} %refs_0_.13, f32[3,3072,768]{2,1,0:T(8,128)} %refs_1_.13, ...), custom_call_target="tpu_custom_call", output_to_operand_aliasing={{0}: (8, {}), {1}: (9, {}), {2}: (10, {})} | custom-call | flops 2123366400 | bytes 66060288 | tf_op jit(solution)/shard_map/lamb/pallas_call | solution.py:349
  828.6 28.3 %lamb.9 = (f32[3,768,3072]{2,1,0:T(8,128)}, f32[3,768,3072]{2,1,0:T(8,128)}, f32[3,768,3072]{2,1,0:T(8,128)}, bf16[768,3072]{1,0:T(8,128)(2,1)}) custom-call(s32[1]{0:T(128)} %bitcast.q_ref.i_ref, f32[3,768,3072]{2,1,0:T(8,128)} %refs_0_.10, f32[3,768,3072]{2,1,0:T(8,128)} %refs_1_.10, ...), custom_call_target="tpu_custom_call", output_to_operand_aliasing={{0}: (8, {}), {1}: (9, {}), {2}: (10, {})} | custom-call | flops 2123366400 | bytes 66060288 | tf_op jit(solution)/shard_map/lamb/pallas_call | solution.py:349
  856.9 28.2 %lamb.13 = (f32[3,3072,768]{2,1,0:T(8,128)}, f32[3,3072,768]{2,1,0:T(8,128)}, f32[3,3072,768]{2,1,0:T(8,128)}, bf16[3072,768]{1,0:T(8,128)(2,1)}) custom-call(s32[1]{0:T(128)} %bitcast.q_ref.i_ref, f32[3,3072,768]{2,1,0:T(8,128)} %refs_0_.13, f32[3,3072,768]{2,1,0:T(8,128)} %refs_1_.13, ...), custom_call_target="tpu_custom_call", output_to_operand_aliasing={{0}: (8, {}), {1}: (9, {}), {2}: (10, {})} | custom-call | flops 2123366400 | bytes 66060288 | tf_op jit(solution)/shard_map/lamb/pallas_call | solution.py:349
  885.0 28.4 %lamb.10 = (f32[3,768,3072]{2,1,0:T(8,128)}, f32[3,768,3072]{2,1,0:T(8,128)}, f32[3,768,3072]{2,1,0:T(8,128)}, bf16[768,3072]{1,0:T(8,128)(2,1)}) custom-call(s32[1]{0:T(128)} %bitcast.q_ref.i_ref, f32[3,768,3072]{2,1,0:T(8,128)} %refs_0_.10, f32[3,768,3072]{2,1,0:T(8,128)} %refs_1_.10, ...), custom_call_target="tpu_custom_call", output_to_operand_aliasing={{0}: (8, {}), {1}: (9, {}), {2}: (10, {})} | custom-call | flops 2123366400 | bytes 66060288 | tf_op jit(solution)/shard_map/lamb/pallas_call | solution.py:349
  913.4 69.4 %forward.1 = f32[2048,768]{1,0:T(8,128)} custom-call(f32[2048,768]{1,0:T(8,128)} %in_matmul.3.h_ref, bf16[768,3072]{1,0:T(8,128)(2,1)} %get-tuple-element.91.refs_0_, bf16[768,3072]{1,0:T(8,128)(2,1)} %get-tuple-element.92.refs_1_, bf16[768,3072]{1,0:T(8,128)(2,1)} %get-tuple-element.93.refs_2_, bf16[3072,768]{1,0:T(8,128)(2,1)} %get-tuple-element.94.refs_3_, ...), custom_call_target="tpu_custom_call" | custom-call | flops 57982058496 | bytes 40894464 | tf_op jit(solution)/shard_map/forward/pallas_call | solution.py:414
  982.8 4.6 multiply_reduce_fusion
  987.5 0.6 broadcast_multiply_fusion
  (41 shorter events, 0.1 us)
Async XLA Ops:
  27.6 207.1 %collective-permute-start.6 = (f32[2048,768]{1,0:T(8,128)}, f32[2048,768]{1,0:T(8,128)}, u32[]{:S(2)}, u32[]{:S(2)}) collective-permute-start(f32[2048,768]{1,0:T(8,128)} %in_matmul.2.h_ref), channel_id=1, source_target_pairs={{0,2},{2,0},{1,3},{3,1},{4,6},{6,4},{5,7},{7,5}} | collective-permute-start | bytes 18874376 | tf_op jit(solution)/shard_map/ppermute | solution.py:445
  30.9 203.8 %collective-permute-start.7 = (bf16[2048,768]{1,0:T(8,128)(2,1)}, bf16[2048,768]{1,0:T(8,128)(2,1)}, u32[]{:S(2)}, u32[]{:S(2)}) collective-permute-start(bf16[2048,768]{1,0:T(8,128)(2,1)} %y_ref.1), channel_id=1, source_target_pairs={{0,2},{2,0},{1,3},{3,1},{4,6},{6,4},{5,7},{7,5}} | collective-permute-start | bytes 9437192 | tf_op jit(solution)/shard_map/ppermute | solution.py:445
  30.9 22.3 %copy-start = (f32[3,3072,768]{2,1,0:T(8,128)S(1)}, f32[3,3072,768]{2,1,0:T(8,128)}, u32[]{:S(2)}) copy-start(f32[3,3072,768]{2,1,0:T(8,128)} %refs_0_.13) | copy-start | bytes 84934656
  209.4 275.1 %collective-permute-start = (bf16[1536,768]{1,0:T(8,128)(2,1)}, bf16[1536,768]{1,0:T(8,128)(2,1)}, u32[]{:S(2)}, u32[]{:S(2)}) collective-permute-start(bf16[1536,768]{1,0:T(8,128)(2,1)} %dwi.5), channel_id=1, source_target_pairs={{0,1},{1,0},{2,3},{3,2},{4,5},{5,4},{6,7},{7,6}} | collective-permute-start | bytes 7077896 | tf_op jit(solution)/shard_map/ppermute | solution.py:445
  218.4 275.2 %collective-permute-start.1 = (bf16[1536,768]{1,0:T(8,128)(2,1)}, bf16[1536,768]{1,0:T(8,128)(2,1)}, u32[]{:S(2)}, u32[]{:S(2)}) collective-permute-start(bf16[1536,768]{1,0:T(8,128)(2,1)} %dwi.6), channel_id=1, source_target_pairs={{0,2},{2,0},{1,3},{3,1},{4,6},{6,4},{5,7},{7,5}} | collective-permute-start | bytes 7077896 | tf_op jit(solution)/shard_map/ppermute | solution.py:445
  229.5 264.0 %collective-permute-start.2 = (bf16[1536,768]{1,0:T(8,128)(2,1)}, bf16[1536,768]{1,0:T(8,128)(2,1)}, u32[]{:S(2)}, u32[]{:S(2)}) collective-permute-start(bf16[1536,768]{1,0:T(8,128)(2,1)} %dwi.7), channel_id=1, source_target_pairs={{0,3},{3,0},{1,2},{2,1},{4,7},{7,4},{5,6},{6,5}} | collective-permute-start | bytes 7077896 | tf_op jit(solution)/shard_map/ppermute | solution.py:445
  448.0 104.5 %collective-permute-start.16 = (f32[2,768,768]{2,1,0:T(8,128)}, f32[2,768,768]{2,1,0:T(8,128)}, u32[]{:S(2)}, u32[]{:S(2)}) collective-permute-start(f32[2,768,768]{2,1,0:T(8,128)} %get-tuple-element.69), channel_id=1, source_target_pairs={{0,1},{1,0},{2,3},{3,2},{4,5},{5,4},{6,7},{7,6}} | collective-permute-start | bytes 14155784 | tf_op jit(solution)/shard_map/ppermute | solution.py:445
  448.0 111.5 %collective-permute-start.12 = (f32[2,768,768]{2,1,0:T(8,128)}, f32[2,768,768]{2,1,0:T(8,128)}, u32[]{:S(2)}, u32[]{:S(2)}) collective-permute-start(f32[2,768,768]{2,1,0:T(8,128)} %get-tuple-element.67), channel_id=1, source_target_pairs={{0,1},{1,0},{2,3},{3,2},{4,5},{5,4},{6,7},{7,6}} | collective-permute-start | bytes 14155784 | tf_op jit(solution)/shard_map/ppermute | solution.py:445
  484.5 79.5 %collective-permute-start.8 = (f32[2,768,768]{2,1,0:T(8,128)}, f32[2,768,768]{2,1,0:T(8,128)}, u32[]{:S(2)}, u32[]{:S(2)}) collective-permute-start(f32[2,768,768]{2,1,0:T(8,128)} %get-tuple-element.65), channel_id=1, source_target_pairs={{0,1},{1,0},{2,3},{3,2},{4,5},{5,4},{6,7},{7,6}} | collective-permute-start | bytes 14155784 | tf_op jit(solution)/shard_map/ppermute | solution.py:445
  493.6 58.9 %copy-start.2 = (f32[2,768,768]{2,1,0:T(8,128)S(1)}, f32[2,768,768]{2,1,0:T(8,128)}, u32[]{:S(2)}) copy-start(f32[2,768,768]{2,1,0:T(8,128)} %get-tuple-element.68) | copy-start | bytes 14155780
  493.6 65.9 %slice-start.2 = ((s8[4718592]{0:T(1024)(128)(4,1)}), s8[4194304]{0:T(1024)(128)(4,1)S(1)}, s32[]{:S(2)}) async-start(s8[4718592]{0:T(1024)(128)(4,1)} %bitcast.3), calls=%async_computation.2 | async-start | bytes 8388608
  498.6 59.1 %copy-start.1 = (bf16[1536,768]{1,0:T(8,128)(2,1)}, bf16[1536,768]{1,0:T(8,128)(2,1)S(1)}, u32[]{:S(2)}) copy-start(bf16[1536,768]{1,0:T(8,128)(2,1)S(1)} %add_convert_fusion.3.refs_3_) | copy-start | bytes 7077892
  498.7 53.8 %collective-permute-start.4 = (bf16[1536,768]{1,0:T(8,128)(2,1)S(1)}, bf16[1536,768]{1,0:T(8,128)(2,1)S(1)}, u32[]{:S(2)}, u32[]{:S(2)}) collective-permute-start(bf16[1536,768]{1,0:T(8,128)(2,1)S(1)} %add_convert_fusion.3.refs_3_), channel_id=1, source_target_pairs={{0,2},{2,0},{1,3},{3,1},{4,6},{6,4},{5,7},{7,5}} | collective-permute-start | bytes 7077896 | tf_op jit(solution)/shard_map/ppermute | solution.py:445
  500.6 68.2 %collective-permute-start.3 = (bf16[1536,768]{1,0:T(8,128)(2,1)S(1)}, bf16[1536,768]{1,0:T(8,128)(2,1)S(1)}, u32[]{:S(2)}, u32[]{:S(2)}) collective-permute-start(bf16[1536,768]{1,0:T(8,128)(2,1)S(1)} %add_convert_fusion.3.refs_3_), channel_id=1, source_target_pairs={{0,1},{1,0},{2,3},{3,2},{4,5},{5,4},{6,7},{7,6}} | collective-permute-start | bytes 7077896 | tf_op jit(solution)/shard_map/ppermute | solution.py:445
  552.4 5.3 copy-start.3
  552.4 59.4 %collective-permute-start.5 = (bf16[1536,768]{1,0:T(8,128)(2,1)S(1)}, bf16[1536,768]{1,0:T(8,128)(2,1)S(1)}, u32[]{:S(2)}, u32[]{:S(2)}) collective-permute-start(bf16[1536,768]{1,0:T(8,128)(2,1)S(1)} %collective-permute-done.4.refs_5_), channel_id=1, source_target_pairs={{0,1},{1,0},{2,3},{3,2},{4,5},{5,4},{6,7},{7,6}} | collective-permute-start | bytes 7077896 | tf_op jit(solution)/shard_map/ppermute | solution.py:445
  552.5 7.0 slice-start.3
  552.5 11.8 %slice-start = ((s8[4718592]{0:T(1024)(128)(4,1)}), s8[4194304]{0:T(1024)(128)(4,1)S(1)}, s32[]{:S(2)}) async-start(s8[4718592]{0:T(1024)(128)(4,1)} %bitcast.1), calls=%async_computation | async-start | bytes 8388608
  557.7 54.1 %collective-permute-start.18 = (bf16[2,768,768]{2,1,0:T(8,128)(2,1)}, bf16[2,768,768]{2,1,0:T(8,128)(2,1)}, u32[]{:S(2)}, u32[]{:S(2)}) collective-permute-start(bf16[2,768,768]{2,1,0:T(8,128)(2,1)} %add_convert_fusion.refs_3_), channel_id=1, source_target_pairs={{0,2},{2,0},{1,3},{3,1},{4,6},{6,4},{5,7},{7,5}} | collective-permute-start | bytes 7077896 | tf_op jit(solution)/shard_map/ppermute | solution.py:445
  559.5 157.3 %collective-permute-start.17 = (bf16[2,768,768]{2,1,0:T(8,128)(2,1)}, bf16[2,768,768]{2,1,0:T(8,128)(2,1)}, u32[]{:S(2)}, u32[]{:S(2)}) collective-permute-start(bf16[2,768,768]{2,1,0:T(8,128)(2,1)} %add_convert_fusion.refs_3_), channel_id=1, source_target_pairs={{0,1},{1,0},{2,3},{3,2},{4,5},{5,4},{6,7},{7,6}} | collective-permute-start | bytes 7077896 | tf_op jit(solution)/shard_map/ppermute | solution.py:445
  559.5 4.8 slice-start.1
  564.0 98.4 %collective-permute-start.14 = (bf16[2,768,768]{2,1,0:T(8,128)(2,1)}, bf16[2,768,768]{2,1,0:T(8,128)(2,1)}, u32[]{:S(2)}, u32[]{:S(2)}) collective-permute-start(bf16[2,768,768]{2,1,0:T(8,128)(2,1)} %add_convert_fusion.1.refs_3_), channel_id=1, source_target_pairs={{0,2},{2,0},{1,3},{3,1},{4,6},{6,4},{5,7},{7,5}} | collective-permute-start | bytes 7077896 | tf_op jit(solution)/shard_map/ppermute | solution.py:445
  568.7 43.2 %copy-start.4 = (bf16[1536,768]{1,0:T(8,128)(2,1)}, bf16[1536,768]{1,0:T(8,128)(2,1)S(1)}, u32[]{:S(2)}) copy-start(bf16[1536,768]{1,0:T(8,128)(2,1)S(1)} %collective-permute-done.3.refs_4_) | copy-start | bytes 7077892
  568.7 148.6 %collective-permute-start.10 = (bf16[2,768,768]{2,1,0:T(8,128)(2,1)}, bf16[2,768,768]{2,1,0:T(8,128)(2,1)}, u32[]{:S(2)}, u32[]{:S(2)}) collective-permute-start(bf16[2,768,768]{2,1,0:T(8,128)(2,1)} %add_convert_fusion.2.refs_3_), channel_id=1, source_target_pairs={{0,2},{2,0},{1,3},{3,1},{4,6},{6,4},{5,7},{7,5}} | collective-permute-start | bytes 7077896 | tf_op jit(solution)/shard_map/ppermute | solution.py:445
  611.9 131.9 %collective-permute-start.19 = (bf16[2,768,768]{2,1,0:T(8,128)(2,1)}, bf16[2,768,768]{2,1,0:T(8,128)(2,1)}, u32[]{:S(2)}, u32[]{:S(2)}) collective-permute-start(bf16[2,768,768]{2,1,0:T(8,128)(2,1)} %collective-permute-done.18.refs_5_), channel_id=1, source_target_pairs={{0,1},{1,0},{2,3},{3,2},{4,5},{5,4},{6,7},{7,6}} | collective-permute-start | bytes 7077896 | tf_op jit(solution)/shard_map/ppermute | solution.py:445
  611.9 1.4 copy-start.5
  611.9 188.6 %collective-permute-start.13 = (bf16[2,768,768]{2,1,0:T(8,128)(2,1)}, bf16[2,768,768]{2,1,0:T(8,128)(2,1)}, u32[]{:S(2)}, u32[]{:S(2)}) collective-permute-start(bf16[2,768,768]{2,1,0:T(8,128)(2,1)} %add_convert_fusion.1.refs_3_), channel_id=1, source_target_pairs={{0,1},{1,0},{2,3},{3,2},{4,5},{5,4},{6,7},{7,6}} | collective-permute-start | bytes 7077896 | tf_op jit(solution)/shard_map/ppermute | solution.py:445
  662.4 138.1 %collective-permute-start.15 = (bf16[2,768,768]{2,1,0:T(8,128)(2,1)}, bf16[2,768,768]{2,1,0:T(8,128)(2,1)}, u32[]{:S(2)}, u32[]{:S(2)}) collective-permute-start(bf16[2,768,768]{2,1,0:T(8,128)(2,1)} %collective-permute-done.14.refs_5_), channel_id=1, source_target_pairs={{0,1},{1,0},{2,3},{3,2},{4,5},{5,4},{6,7},{7,6}} | collective-permute-start | bytes 7077896 | tf_op jit(solution)/shard_map/ppermute | solution.py:445
  716.8 140.0 %collective-permute-start.9 = (bf16[2,768,768]{2,1,0:T(8,128)(2,1)}, bf16[2,768,768]{2,1,0:T(8,128)(2,1)}, u32[]{:S(2)}, u32[]{:S(2)}) collective-permute-start(bf16[2,768,768]{2,1,0:T(8,128)(2,1)} %add_convert_fusion.2.refs_3_), channel_id=1, source_target_pairs={{0,1},{1,0},{2,3},{3,2},{4,5},{5,4},{6,7},{7,6}} | collective-permute-start | bytes 7077896 | tf_op jit(solution)/shard_map/ppermute | solution.py:445
  717.3 139.6 %collective-permute-start.11 = (bf16[2,768,768]{2,1,0:T(8,128)(2,1)}, bf16[2,768,768]{2,1,0:T(8,128)(2,1)}, u32[]{:S(2)}, u32[]{:S(2)}) collective-permute-start(bf16[2,768,768]{2,1,0:T(8,128)(2,1)} %collective-permute-done.10.refs_5_), channel_id=1, source_target_pairs={{0,1},{1,0},{2,3},{3,2},{4,5},{5,4},{6,7},{7,6}} | collective-permute-start | bytes 7077896 | tf_op jit(solution)/shard_map/ppermute | solution.py:445

commit v2 on v1

--- a/solution.py
+++ b/solution.py
@@ -6,6 +6,7 @@
 from jax.experimental import pallas as pl
 from jax.experimental.pallas import tpu as pltpu
 from jax.sharding import PartitionSpec as P
+
 
 BETA1 = 0.9
 BETA2 = 0.999
@@ -34,10 +35,6 @@
     return lax.dot_general(a, b, (((1,), (1,)), ((), ())), preferred_element_type=F32)
 
 
-def dot_tn(a, b):
-    return lax.dot_general(a, b, (((0,), (0,)), ((), ())), preferred_element_type=F32)
-
-
 def gelu(a):
     return (0.5 * a) * (1.0 + lax.erf(a * R2))
 
@@ -73,12 +70,11 @@
         out_shape=jax.ShapeDtypeStruct((t, d), F32),
         compiler_params=params("arbitrary"),
         cost_estimate=cost(2 * t * e * d, 2 * t * e + w.nbytes + 4 * t * d),
-        name="in_matmul",
     )(x, w)
 
 
 def chain_kernel(scale, dev, nm, c_ref, h_ref, y_ref, w1_hbm, w2_hbm, *rest):
-    hb_o, s_o, gb_o, e_o, g0_o, w1, w2, a_s, s_s, h_s, sem = rest[4 * (dev > 0):]
+    t_o, p_o, g0_o, w1, w2, a_s, s_s, h_s, b_s, sem = rest[2 * (dev > 0):]
     t = pl.program_id(0)
     c = c_ref[0]
     nl, _, f = w1.shape
@@ -103,8 +99,8 @@
 
     h_s[...] = h_ref[...]
 
-    def piece(o, l, j):
-        return o.at[0, l, :, j * fc:(j + 1) * fc] if j < nm else s_s.at[:, (j - nm) * fc:(j - nm + 1) * fc]
+    def piece(l, kind, j):
+        return p_o.at[0, l, kind, :, j * fc:(j + 1) * fc] if j < nm else s_s.at[:, (j - nm) * fc:(j - nm + 1) * fc]
 
     def fwd(l, carry):
         @pl.when(t == 0)
@@ -112,38 +108,40 @@
             for cp in copies(l):
                 cp.wait()
 
-        hb_o[0, l] = h_s[...].astype(BF)
+        b_s[...] = h_s[...].astype(BF)
 
         def up(j):
-            a_s[l, :, j * fc:(j + 1) * fc] = dot(hb_o[0, l], w1[l, :, j * fc:(j + 1) * fc])
+            a_s[l, :, j * fc:(j + 1) * fc] = dot(b_s[...], w1[l, :, j * fc:(j + 1) * fc])
 
         up(0)
+        t_o[0, l, 1] = b_s[...].T
         for j in range(2 * nm):
             if j + 1 < 2 * nm:
                 up(j + 1)
-            piece(s_o, l, j)[...] = gelu(a_s[l, :, j * fc:(j + 1) * fc]).astype(BF)
-            h_s[...] += dot(piece(s_o, l, j)[...], w2[l, j * fc:(j + 1) * fc, :])
+            piece(l, 0, j)[...] = gelu(a_s[l, :, j * fc:(j + 1) * fc]).astype(BF)
+            h_s[...] += dot(piece(l, 0, j)[...], w2[l, j * fc:(j + 1) * fc, :])
         return carry
 
     def bwd(k, carry):
         l = nl - 1 - k
-        gb_o[0, l] = h_s[...].astype(BF)
+        b_s[...] = h_s[...].astype(BF)
 
         def down(j):
-            return dot_nt(gb_o[0, l], w2[l, j * fc:(j + 1) * fc, :])
+            return dot_nt(b_s[...], w2[l, j * fc:(j + 1) * fc, :])
 
         de = down(0)
+        t_o[0, l, 0] = b_s[...].T
         for j in range(2 * nm):
             nxt = down(j + 1) if j + 1 < 2 * nm else None
-            piece(e_o, l, j)[...] = (de * gelu_grad(a_s[l, :, j * fc:(j + 1) * fc])).astype(BF)
-            h_s[...] += dot_nt(piece(e_o, l, j)[...], w1[l, :, j * fc:(j + 1) * fc])
+            piece(l, 1, j)[...] = (de * gelu_grad(a_s[l, :, j * fc:(j + 1) * fc])).astype(BF)
+            h_s[...] += dot_nt(piece(l, 1, j)[...], w1[l, :, j * fc:(j + 1) * fc])
             de = nxt
         return carry
 
     lax.fori_loop(0, nl, fwd, 0)
     h_s[...] = (h_s[...] - y_ref[...].astype(F32)) * scale
     lax.fori_loop(0, nl, bwd, 0)
-    g0_o[...] = h_s[...].astype(BF)
+    g0_o[...] = h_s[...].astype(BF).T
 
 
 def chain(c, h, y, w1, w2, scale, prev=None, tm=256, nm=2):
@@ -152,126 +150,96 @@
     half = f // 2
     dev = 0 if prev is None else 1
     tok = pl.BlockSpec((tm, d), lambda i, c: (i, 0))
-
-    def out(w):
-        return pl.BlockSpec((1, nl, tm, w), lambda i, c: (dev, 0, i, 0))
-
-    shapes = [jax.ShapeDtypeStruct((2, nl, t, w), BF) for w in (d, half, d, half)]
     return pl.pallas_call(
         functools.partial(chain_kernel, scale, dev, nm),
         grid_spec=pltpu.PrefetchScalarGridSpec(
             num_scalar_prefetch=1,
             grid=(t // tm,),
-            in_specs=[tok, tok, ANY, ANY] + [ANY] * (4 * dev),
-            out_specs=[out(d), out(half), out(d), out(half), tok],
+            in_specs=[tok, tok, ANY, ANY] + [ANY] * (2 * dev),
+            out_specs=[pl.BlockSpec((1, nl, 2, d, tm), lambda i, c: (dev, 0, 0, 0, i)),
+                       pl.BlockSpec((1, nl, 2, tm, half), lambda i, c: (dev, 0, 0, i, 0)),
+                       pl.BlockSpec((d, tm), lambda i, c: (0, i))],
             scratch_shapes=[
                 pltpu.VMEM((nl, d, f), BF),
                 pltpu.VMEM((nl, f, d), BF),
                 pltpu.VMEM((nl, tm, f), F32),
                 pltpu.VMEM((tm, half), BF),
                 pltpu.VMEM((tm, d), F32),
+                pltpu.VMEM((tm, d), BF),
                 pltpu.SemaphoreType.DMA((nl, 4)),
             ],
         ),
-        out_shape=shapes + [jax.ShapeDtypeStruct((t, d), BF)],
-        input_output_aliases={5 + k: k for k in range(4 * dev)},
+        out_shape=[jax.ShapeDtypeStruct((2, nl, 2, d, t), BF), jax.ShapeDtypeStruct((2, nl, 2, t, half), BF),
+                   jax.ShapeDtypeStruct((d, t), BF)],
+        input_output_aliases={5 + k: k for k in range(2 * dev)},
         compiler_params=params("arbitrary"),
         cost_estimate=cost(8 * nl * t * d * f, 4 * nl * d * f + 8 * t * d + 4 * nl * t * (d + half)),
-        name="chain_%d" % dev,
     )(c, h, y, w1, w2, *(prev or ()))
 
 
-def dw_kernel(i_ref, hb_ref, s_ref, gb_ref, e_ref, sp_o, sm_o, acc):
-    job, dev, k = pl.program_id(0), pl.program_id(1), pl.program_id(2)
-    nk = pl.num_programs(2)
-
-    def product(a_ref, b_ref):
-        acc[...] = jnp.where(k == 0, 0.0, acc[...]) + dot_tn(a_ref[0, 0], b_ref[0, 0])
-
-    @pl.when(job % 2 == 0)
-    def _():
-        product(s_ref, gb_ref)
-
-    @pl.when(job % 2 == 1)
-    def _():
-        product(hb_ref, e_ref)
-
-    def add(o):
-        r = acc[...].astype(BF).astype(F32)
-        o[0] = jnp.where(dev == 0, 0.0, o[0]) + r
-
-    @pl.when((k == nk - 1) & (job < 2))
-    def _():
-        add(sp_o)
-
-    @pl.when((k == nk - 1) & (job >= 2))
-    def _():
-        add(sm_o)
-
-
-def dw_half(core, acts, l, kb=1024):
-    hb, s, gb, e = acts
-    t, d = hb.shape[2:]
-    q = s.shape[3] // 2
-
-    def quarter(job, core):
-        return jnp.where(job < 2, 1 - core, core)
-
-    def feat(odd):
-        def index(job, dev, k, c):
-            mine = job % 2 == odd
-            return (jnp.where(mine, dev, 0), l, jnp.where(mine, k, 0), quarter(job, c[0]))
-        return index
-
-    def full(odd):
-        def index(job, dev, k, c):
-            mine = job % 2 == odd
-            return (jnp.where(mine, dev, 0), l, jnp.where(mine, k, 0), 0)
-        return index
-
-    blk = (1, 1, kb, q)
+def dw_kernel(i_ref, t_ref, p_ref, o_ref):
+    r = dot(t_ref[0, 0, 0], p_ref[0, 0, 0]).astype(BF).astype(F32)
+    o_ref[0] = jnp.where(pl.program_id(1) == 0, 0.0, o_ref[0]) + r
+
+
+def dw_half(core, acts, l):
+    ts, ps = acts
+    d, t = ts.shape[3:]
+    q = ps.shape[4] // 2
     return pl.pallas_call(
         dw_kernel,
         grid_spec=pltpu.PrefetchScalarGridSpec(
             num_scalar_prefetch=1,
-            grid=(4, 2, t // kb),
-            in_specs=[pl.BlockSpec((1, 1, kb, d), full(1)), pl.BlockSpec(blk, feat(0)),
-                      pl.BlockSpec((1, 1, kb, d), full(0)), pl.BlockSpec(blk, feat(1))],
-            out_specs=[pl.BlockSpec((1, d, d), lambda job, dev, k, c: (jnp.minimum(job, 1), 0, 0)),
-                       pl.BlockSpec((1, d, d), lambda job, dev, k, c: (jnp.maximum(job - 2, 0), 0, 0))],
-            scratch_shapes=[pltpu.VMEM((d, d), F32)],
+            grid=(4, 2),
+            in_specs=[pl.BlockSpec((1, 1, 1, d, t), lambda job, dev, c: (dev, l, job % 2, 0, 0)),
+                      pl.BlockSpec((1, 1, 1, t, q), lambda job, dev, c: (
+                          dev, l, job % 2, 0, jnp.where(job < 2, 1 - c[0], c[0])))],
+            out_specs=pl.BlockSpec((1, d, q), lambda job, dev, c: (job, 0, 0)),
         ),
-        out_shape=[jax.ShapeDtypeStruct((2, d, d), F32)] * 2,
-        compiler_params=params("arbitrary", "arbitrary", "arbitrary"),
-        cost_estimate=cost(16 * t * d * d, 16 * t * d * 2 + 16 * d * d),
-        name="dw_%d" % l,
-    )(core, hb, s, gb, e)
-
-
-def dwi_kernel(q_ref, x_ref, g_ref, o_ref):
-    o_ref[...] = dot_tn(x_ref[...], g_ref[...]).astype(BF)
-
-
-def dwi_quarter(q, x, g, mb=512):
+        out_shape=jax.ShapeDtypeStruct((4, d, q), F32),
+        compiler_params=params("arbitrary", "arbitrary"),
+        cost_estimate=cost(16 * t * d * q, 16 * t * (d + q) + 16 * d * q),
+    )(core, ts, ps)
+
+
+def dwi_kernel(i_ref, g_ref, x_ref, *refs):
+    acc = refs[-1]
+    acc[...] = dot(g_ref[...], x_ref[...])
+    for k in range(4):
+        @pl.when(pl.program_id(0) == k)
+        def _(k=k):
+            refs[k][...] = acc[...].astype(BF)
+
+
+def dwi_quarters(i, g, x, eb=512):
     t, e = x.shape
-    d = g.shape[1]
-    n = e // 4 // mb
+    d = g.shape[0]
+    n = e // 4 // eb
+
+    def quarter(k, i):
+        return jnp.bitwise_xor(jnp.where(k == 0, 2, jnp.where(k == 1, 3, jnp.where(k == 2, 1, 0))), i[0])
+
+    def at(kk):
+        return lambda k, j, i: (0, jnp.where(k < kk, 0, jnp.where(k > kk, n - 1, j)))
+
     return pl.pallas_call(
         dwi_kernel,
         grid_spec=pltpu.PrefetchScalarGridSpec(
             num_scalar_prefetch=1,
-            grid=(n,),
-            in_specs=[pl.BlockSpec((t, mb), lambda j, q: (0, q[0] * n + j)), pl.BlockSpec((t, d), lambda j, q: (0, 0))],
-            out_specs=pl.BlockSpec((mb, d), lambda j, q: (j, 0)),
+            grid=(4, n),
+            in_specs=[pl.BlockSpec((d, t), lambda k, j, i: (0, 0)),
+                      pl.BlockSpec((t, eb), lambda k, j, i: (0, quarter(k, i) * n + j))],
+            out_specs=[pl.BlockSpec((d, eb), at(kk)) for kk in range(4)],
+            scratch_shapes=[pltpu.VMEM((d, eb), F32)],
         ),
-        out_shape=jax.ShapeDtypeStruct((e // 4, d), BF),
-        compiler_params=params("arbitrary"),
-        cost_estimate=cost(2 * t * e * d // 4, t * e // 2 + 2 * t * d),
+        out_shape=[jax.ShapeDtypeStruct((d, e // 4), BF)] * 4,
+        compiler_params=params("arbitrary", "arbitrary"),
+        cost_estimate=cost(2 * t * e * d, 2 * t * (e + d) + 2 * d * e),
         name="dwi",
-    )(q, x, g)
-
-
-def lamb_kernel(nb, gi, i_ref, *refs):
+    )(i, g, x)
+
+
+def lamb_kernel(nb, flip, i_ref, *refs):
     w_ref, m_ref, v_ref, g0, g1, g2, g3 = refs[:7]
     wn_o, mn_o, vn_o, wb_o, w_s, u_s, sw, su, ratio = refs[-9:]
     p, k, j = pl.program_id(0), pl.program_id(1), pl.program_id(2)
@@ -286,7 +254,8 @@
 
     def sweep(g_ref):
         w = w_ref[...].reshape(shape)
-        g = g_ref[...].reshape(shape).astype(F32)
+        g = g_ref[...].reshape(g_ref.shape[-2:]).astype(F32)
+        g = g.T if flip else g
         m2 = BETA1 * m_ref[...].reshape(shape) + (1.0 - BETA1) * g
         v2 = BETA2 * v_ref[...].reshape(shape) + (1.0 - BETA2) * g * g
         u = BC1 * m2 / (jnp.sqrt(BC2 * v2) + EPS) + WD * w
@@ -315,39 +284,42 @@
 
 def lamb(i, w, m, v, gs, gi, l, bufs, cols, rb):
     rows, width = w.shape[-2:]
-    gr, gw = gs[0].shape[-2:]
+    gr, gw = gs[0].shape[-2:] if cols else gs[0].shape[:-3:-1]
     nb = gr // rb
     lead = () if l is None else (l,)
     one = () if l is None else (1,)
 
-    def where(p, k, j, i):
+    def where(k, j, i):
         q = jnp.bitwise_xor(k, i[0])
         return (j, q) if cols else (q * nb + j, 0)
 
     def at_first(p, k, j, i):
         k, j = jnp.where(p == 0, k, 3), jnp.where(p == 0, j, nb - 1)
-        return lead + where(p, k, j, i)
+        return lead + where(k, j, i)
 
     def at_second(p, k, j, i):
         k, j = jnp.where(p == 1, k, 0), jnp.where(p == 1, j, 0)
-        return lead + where(p, k, j, i)
+        return lead + where(k, j, i)
 
     def at_second2(p, k, j, i):
         k, j = jnp.where(p == 1, k, 0), jnp.where(p == 1, j, 0)
-        return where(p, k, j, i)
+        return where(k, j, i)
 
     def at_g(kk):
         def index(p, k, j, i):
             b = jnp.where((p == 1) | (k > kk), nb - 1, jnp.where(k < kk, 0, j))
-            return (b, 0) if gi is None else (gi, b, 0)
+            b = (b, 0) if cols else (0, b)
+            return b if gi is None else (gi,) + b
+
         return index
 
     blk = one + (rb, gw)
-    gblk = (rb, gw) if gi is None else (1, rb, gw)
+    gblk = (rb, gw) if cols else (gw, rb)
+    gblk = gblk if gi is None else (1,) + gblk
     n = len(bufs)
     f32 = jax.ShapeDtypeStruct(w.shape, F32)
     return pl.pallas_call(
-        functools.partial(lamb_kernel, nb, gi),
+        functools.partial(lamb_kernel, nb, not cols),
         grid_spec=pltpu.PrefetchScalarGridSpec(
             num_scalar_prefetch=1,
             grid=(2, 4, nb),
@@ -366,7 +338,6 @@
         input_output_aliases={8 + k: k for k in range(n)},
         compiler_params=params("arbitrary", "arbitrary", "arbitrary"),
         cost_estimate=cost(30 * rows * width * 30, 28 * rows * width),
-        name="lamb",
     )(i, w, m, v, *gs, *bufs)
 
 
@@ -433,8 +404,8 @@
 def solution(mesh):
     p = mesh.shape['data']
 
-    def step(wi, w1, w2, mi, vi, m1, v1, m2, v2, x0, y0, x1, y1):
-        nl, d, f = w1.shape
+    def inner(wi, w1, w2, mi, vi, m1, v1, m2, v2, x0, y0, x1, y1):
+        nl, d, _ = w1.shape
         scale = 1.0 / (x0.shape[0] * p * d)
         i = lax.axis_index('data').astype(jnp.int32)
         me = jnp.reshape(i, (1,))
@@ -448,20 +419,26 @@
             far = send(g, CROSS)
             return g, send(g, D2D), far, send(far, D2D)
 
-        w1b, w2b = w1.astype(BF), w2.astype(BF)
         y0o = send(y0, CROSS)
         h0 = in_matmul(x0, wi)
         h0o = send(h0, CROSS)
+        w1b, w2b = w1.astype(BF), w2.astype(BF)
         *acts, g0 = chain(chip, h0, y0, w1b, w2b, scale)
-        pieces = {k: dwi_quarter(jnp.bitwise_xor(me, k), x0, g0) for k in (2, 3, 1, 0)}
-        got = [pieces[0], send(pieces[1], D2D), send(pieces[2], CROSS), send(pieces[3], DIAG)]
+        *far, near, own = dwi_quarters(me, g0, x0)
+        got = [own, send(near, D2D), send(far[0], CROSS), send(far[1], DIAG)]
+        *acts, _ = chain(chip, h0o, y0o, w1b, w2b, scale, lax.optimization_barrier((acts, own))[0])
+        got, acts = lax.optimization_barrier((got, acts))
         si = sum(g.astype(F32) for g in got).astype(BF)
         gi = gather(si)
-        *acts, _ = chain(chip, h0o, y0o, w1b, w2b, scale, acts)
         gl = []
         for l in range(nl):
-            sp, sm = dw_half(core, acts, l)
-            gl.append(gather((sm + send(sp, D2D)).astype(BF)))
+            acts = lax.optimization_barrier((acts, si if l == 0 else parts if l == 1 else gl[-1][0]))[0]
+            last = parts if l else None
+            parts = dw_half(core, acts, l)
+            if l:
+                gl.append(gather((last[2:] + other[:2]).astype(BF)))
+            other = send(parts, D2D)
+        gl.append(gather((parts[2:] + other[:2]).astype(BF)))
         wi_n, mi_n, vi_n, wib = lamb(me, wi, mi, vi, gi, None, None, (), False, 384)
         b1, b2 = (), ()
         w1n, w2n = [], []
@@ -477,7 +454,7 @@
     w2s = P('rep', None)
     w3s = P('rep', None, None)
     ts = P(('rep', 'data'), None)
-    return jax.shard_map(step, mesh=mesh,
+    return jax.shard_map(inner, mesh=mesh,
                          in_specs=(w2s, w3s, w3s, w2s, w2s, w3s, w3s, w3s, w3s, ts, ts, ts, ts),
                          out_specs=(w2s, w3s, w3s, w2s, w2s, w3s, w3s, w3s, w3s, P(('rep', 'data')), ts),
                          check_vma=False)

time: 997 us -> 964 us (0.967)
  Pallas kernels: 773 us -> 740 us
    pallas_call x3, Pallas kernels: 108 us -> 86 us  [dw_half(): pl.pallas_call(dw_kernel, grid_spec=pltpu.PrefetchScalarGridSpec(num_scal...]
    pallas_call x11 -> x8, Pallas kernels: 260 us -> 247 us  [the longest x7 220 us: lamb(): pl.pallas_call(functools.partial(lamb_kernel, nb, not cols), grid_spec=pl...]
  transfers between devices with their start and end apart: 20 -> 20, of which waited for: 4 -> 4; matrix products, arithmetic and copies ran while one was open for 4% -> 4% of each run, Pallas kernels for 63% -> 58%
where the time goes in v2:
time: 964 us; the launch traced here: 956 us
  Pallas kernels  740 us (77%)
  waiting for transfers between devices  148 us (15%)
  other arithmetic  47 us (5%)
  starting transfers between devices  13.3 us (1%)
    pallas_call x2, Pallas kernels, chain(): pl.pallas_call(functools.partial(chain_kernel, scale, dev, nm), grid_spec...  283 us
    pallas_call x7, Pallas kernels, lamb(): pl.pallas_call(functools.partial(lamb_kernel, nb, not cols), grid_spec=pl...  220 us
    ppermute x20, waiting for transfers between devices, send(): return lax.ppermute(x, 'data', perm)  148 us
    pallas_call x3, Pallas kernels, dw_half(): pl.pallas_call(dw_kernel, grid_spec=pltpu.PrefetchScalarGridSpec(num_scal...  86 us
    pallas_call x1, Pallas kernels, forward(): pl.pallas_call(functools.partial(fwd_kernel, nl, nj), grid=(t // tm,), in...  69.5 us
    pallas_call x2, Pallas kernels, in_matmul(): pl.pallas_call(in_kernel, grid=(e // kb,), in_specs=[pl.BlockSpec((t, kb)...  53.3 us
    pallas_call x1, Pallas kernels, dwi_quarters(): pl.pallas_call(dwi_kernel, grid_spec=pltpu.PrefetchScalarGridSpec(num_sca...  27.8 us
    convert_element_type x2, other arithmetic, inner(): w1b, w2b = (w1.astype(BF), w2.astype(BF))  22.2 us
  transfers between devices with their start and end apart: 20, of which 4 were waited for; matrix products, arithmetic and copies ran while one was open for 4% of the time, Pallas kernels for 58%

profile of v2, /device:TPU:0, one launch (start us, length us, event | category | flops | bytes accessed | tf_op | source)
XLA Modules:
  0.0 956.1 jit_solution(8982605880101384072)
XLA Ops:
  0.6 26.9 %shard_map.212.h_ref = f32[2048,768]{1,0:T(8,128)} custom-call(bf16[2048,6144]{1,0:T(8,128)(2,1)} %x_ref.4, f32[6144,768]{1,0:T(8,128)} %refs_0_.7), custom_call_target="tpu_custom_call" | custom-call | flops 19327352832 | bytes 50331648 | tf_op jit(solution)/shard_map/pallas_call | solution.py:65
  27.6 3.3 collective-permute-start.3
  30.9 0.0 collective-permute-start.4
  30.9 16.2 %convert_element_type.33.w1_hbm = bf16[3,768,3072]{2,1,0:T(8,128)(2,1)} convert(f32[3,768,3072]{2,1,0:T(8,128)} %refs_0_.10) | non-fusion elementwise | flops 7077888 | bytes 42467328 | tf_op jit(solution)/shard_map/convert_element_type | solution.py:425
  47.1 6.1 copy-done
  53.2 6.0 convert_element_type.34.w2_hbm
  59.1 141.6 %shard_map.213 = (bf16[2,3,2,768,2048]{4,3,2,1,0:T(8,128)(2,1)}, bf16[2,3,2,2048,1536]{4,3,2,1,0:T(8,128)(2,1)}, bf16[768,2048]{1,0:T(8,128)(2,1)}) custom-call(s32[1]{0:T(128)S(6)} %select_n.12.c_ref, f32[2048,768]{1,0:T(8,128)} %shard_map.212.h_ref, bf16[2048,768]{1,0:T(8,128)(2,1)} %y_ref.1, bf16[3,768,3072]{2,1,0:T(8,128)(2,1)} %convert_element_type.33.w1_hbm, ...), custom_call_target="tpu_custom_call" | custom-call | flops 115964116992 | bytes 97517568 | tf_op jit(solution)/shard_map/pallas_call | solution.py:153
  200.7 27.8 %dwi.1 = (bf16[768,1536]{1,0:T(8,128)(2,1)}, bf16[768,1536]{1,0:T(8,128)(2,1)}, bf16[768,1536]{1,0:T(8,128)(2,1)}, bf16[768,1536]{1,0:T(8,128)(2,1)}) custom-call(s32[1]{0:T(128)} %bitcast.i_ref, bf16[768,2048]{1,0:T(8,128)(2,1)} %get-tuple-element.62.g_ref, bf16[2048,6144]{1,0:T(8,128)(2,1)} %x_ref.4), custom_call_target="tpu_custom_call" | custom-call | flops 19327352832 | bytes 37748736 | tf_op jit(solution)/shard_map/dwi/pallas_call | solution.py:225
  228.6 2.0 collective-permute-start.1
  230.6 0.1 collective-permute-start.2
  230.7 4.3 collective-permute-done.4.y_ref
  235.0 141.9 %shard_map.214 = (bf16[2,3,2,768,2048]{4,3,2,1,0:T(8,128)(2,1)}, bf16[2,3,2,2048,1536]{4,3,2,1,0:T(8,128)(2,1)}, bf16[768,2048]{1,0:T(8,128)(2,1)}) custom-call(s32[1]{0:T(128)S(6)} %select_n.12.c_ref, f32[2048,768]{1,0:T(8,128)} %collective-permute-done.3.h_ref, ...), custom_call_target="tpu_custom_call", output_to_operand_aliasing={{0}: (5, {}), {1}: (6, {})} | custom-call | flops 115964116992 | bytes 97517568 | tf_op jit(solution)/shard_map/pallas_call | solution.py:153
  376.9 0.0 collective-permute-done.1
  376.9 0.0 collective-permute-done.2
  376.9 6.4 add_convert_fusion.refs_3_
  383.3 28.5 %shard_map.216 = f32[4,768,768]{2,1,0:T(8,128)} custom-call(s32[1]{0:T(128)S(6)} %select_n.13.i_ref, bf16[2,3,2,768,2048]{4,3,2,1,0:T(8,128)(2,1)} %get-tuple-element.84.t_ref, bf16[2,3,2,2048,1536]{4,3,2,1,0:T(8,128)(2,1)} %get-tuple-element.85.p_ref), custom_call_target="tpu_custom_call" | custom-call | flops 19327352832 | bytes 59768832 | tf_op jit(solution)/shard_map/pallas_call | solution.py:189
  411.8 28.5 %shard_map.218 = f32[4,768,768]{2,1,0:T(8,128)} custom-call(s32[1]{0:T(128)S(6)} %select_n.13.i_ref, bf16[2,3,2,768,2048]{4,3,2,1,0:T(8,128)(2,1)} %get-tuple-element.84.t_ref, bf16[2,3,2,2048,1536]{4,3,2,1,0:T(8,128)(2,1)} %get-tuple-element.85.p_ref), custom_call_target="tpu_custom_call" | custom-call | flops 19327352832 | bytes 59768832 | tf_op jit(solution)/shard_map/pallas_call | solution.py:189
  440.3 0.5 collective-permute-start.13
  440.8 5.7 fusion.2.refs_3_
  446.4 29.0 %shard_map.217 = f32[4,768,768]{2,1,0:T(8,128)} custom-call(s32[1]{0:T(128)S(6)} %select_n.13.i_ref, bf16[2,3,2,768,2048]{4,3,2,1,0:T(8,128)(2,1)} %get-tuple-element.84.t_ref, bf16[2,3,2,2048,1536]{4,3,2,1,0:T(8,128)(2,1)} %get-tuple-element.85.p_ref), custom_call_target="tpu_custom_call" | custom-call | flops 19327352832 | bytes 59768832 | tf_op jit(solution)/shard_map/pallas_call | solution.py:189
  475.5 0.0 collective-permute-start.9
  475.5 2.0 collective-permute-start.6
  477.5 0.2 collective-permute-start.5
  477.7 51.9 %collective-permute-done.6.refs_5_ = bf16[768,1536]{1,0:T(8,128)(2,1)S(1)} collective-permute-done((bf16[768,1536]{1,0:T(8,128)(2,1)}, bf16[768,1536]{1,0:T(8,128)(2,1)S(1)}, u32[]{:S(2)}, u32[]{:S(2)}) %collective-permute-start.6) | collective-permute-done | bytes 2359328 | tf_op jit(solution)/shard_map/ppermute | solution.py:416
  529.6 1.7 collective-permute-start.18
  531.4 0.2 collective-permute-start.17
  531.6 5.7 fusion.refs_3_
  537.3 0.6 collective-permute-start.15
  537.8 1.9 fusion.1.refs_3_
  539.7 1.5 collective-permute-start.11
  541.2 42.8 %collective-permute-done.18.refs_5_ = bf16[2,768,768]{2,1,0:T(8,128)(2,1)} collective-permute-done((bf16[2,768,768]{2,1,0:T(8,128)(2,1)}, bf16[2,768,768]{2,1,0:T(8,128)(2,1)}, u32[]{:S(2)}, u32[]{:S(2)}) %collective-permute-start.18) | collective-permute-done | bytes 2359328 | tf_op jit(solution)/shard_map/ppermute | solution.py:416
  584.1 0.0 copy-start.4
  584.1 0.5 collective-permute-start.14
  584.6 0.9 copy-done.4
  585.5 49.1 %collective-permute-done.15.refs_5_ = bf16[2,768,768]{2,1,0:T(8,128)(2,1)} collective-permute-done((bf16[2,768,768]{2,1,0:T(8,128)(2,1)}, bf16[2,768,768]{2,1,0:T(8,128)(2,1)}, u32[]{:S(2)}, u32[]{:S(2)}) %collective-permute-start.15) | collective-permute-done | bytes 2359328 | tf_op jit(solution)/shard_map/ppermute | solution.py:416
  634.6 52.9 %shard_map.215 = (f32[6144,768]{1,0:T(8,128)}, f32[6144,768]{1,0:T(8,128)}, f32[6144,768]{1,0:T(8,128)}, bf16[6144,768]{1,0:T(8,128)(2,1)}) custom-call(s32[1]{0:T(128)} %bitcast.i_ref, f32[6144,768]{1,0:T(8,128)} %refs_0_.7, f32[6144,768]{1,0:T(8,128)} %refs_1_.7, f32[6144,768]{1,0:T(8,128)} %refs_2_.7, bf16[768,1536]{1,0:T(8,128)(2,1)} %add_convert_fusion.refs_3_, ...), custom_call_target="tpu_custom_call" | custom-call | flops 4246732800 | bytes 132120576 | tf_op jit(solution)/shard_map/pallas_call | solution.py:321
  687.5 0.3 collective-permute-start.10
  687.8 0.2 collective-permute-start.12
  688.0 26.4 %shard_map.225.h_ref = f32[2048,768]{1,0:T(8,128)} custom-call(bf16[2048,6144]{1,0:T(8,128)(2,1)} %x_ref.5, bf16[6144,768]{1,0:T(8,128)(2,1)} %get-tuple-element.106.w_ref), custom_call_target="tpu_custom_call" | custom-call | flops 19327352832 | bytes 40894464 | tf_op jit(solution)/shard_map/pallas_call | solution.py:65
  714.4 27.4 %shard_map.222 = (f32[3,3072,768]{2,1,0:T(8,128)}, f32[3,3072,768]{2,1,0:T(8,128)}, f32[3,3072,768]{2,1,0:T(8,128)}, bf16[3072,768]{1,0:T(8,128)(2,1)}) custom-call(s32[1]{0:T(128)} %bitcast.i_ref, f32[3,3072,768]{2,1,0:T(8,128)} %refs_0_.13, f32[3,3072,768]{2,1,0:T(8,128)} %refs_1_.13, f32[3,3072,768]{2,1,0:T(8,128)} %refs_2_.13, ...), custom_call_target="tpu_custom_call" | custom-call | flops 2123366400 | bytes 66060288 | tf_op jit(solution)/shard_map/pallas_call | solution.py:321
  741.8 28.1 %shard_map.219 = (f32[3,768,3072]{2,1,0:T(8,128)}, f32[3,768,3072]{2,1,0:T(8,128)}, f32[3,768,3072]{2,1,0:T(8,128)}, bf16[768,3072]{1,0:T(8,128)(2,1)}) custom-call(s32[1]{0:T(128)} %bitcast.i_ref, f32[3,768,3072]{2,1,0:T(8,128)} %refs_0_.10, f32[3,768,3072]{2,1,0:T(8,128)} %refs_1_.10, f32[3,768,3072]{2,1,0:T(8,128)} %refs_2_.10, ...), custom_call_target="tpu_custom_call" | custom-call | flops 2123366400 | bytes 66060288 | tf_op jit(solution)/shard_map/pallas_call | solution.py:321
  770.0 27.5 %shard_map.223 = (f32[3,3072,768]{2,1,0:T(8,128)}, f32[3,3072,768]{2,1,0:T(8,128)}, f32[3,3072,768]{2,1,0:T(8,128)}, bf16[3072,768]{1,0:T(8,128)(2,1)}) custom-call(s32[1]{0:T(128)} %bitcast.i_ref, f32[3,3072,768]{2,1,0:T(8,128)} %refs_0_.13, f32[3,3072,768]{2,1,0:T(8,128)} %refs_1_.13, ...), custom_call_target="tpu_custom_call", output_to_operand_aliasing={{0}: (8, {}), {1}: (9, {}), {2}: (10, {})} | custom-call | flops 2123366400 | bytes 66060288 | tf_op jit(solution)/shard_map/pallas_call | solution.py:321
  797.5 28.0 %shard_map.220 = (f32[3,768,3072]{2,1,0:T(8,128)}, f32[3,768,3072]{2,1,0:T(8,128)}, f32[3,768,3072]{2,1,0:T(8,128)}, bf16[768,3072]{1,0:T(8,128)(2,1)}) custom-call(s32[1]{0:T(128)} %bitcast.i_ref, f32[3,768,3072]{2,1,0:T(8,128)} %refs_0_.10, f32[3,768,3072]{2,1,0:T(8,128)} %refs_1_.10, ...), custom_call_target="tpu_custom_call", output_to_operand_aliasing={{0}: (8, {}), {1}: (9, {}), {2}: (10, {})} | custom-call | flops 2123366400 | bytes 66060288 | tf_op jit(solution)/shard_map/pallas_call | solution.py:321
  825.5 27.6 %shard_map.224 = (f32[3,3072,768]{2,1,0:T(8,128)}, f32[3,3072,768]{2,1,0:T(8,128)}, f32[3,3072,768]{2,1,0:T(8,128)}, bf16[3072,768]{1,0:T(8,128)(2,1)}) custom-call(s32[1]{0:T(128)} %bitcast.i_ref, f32[3,3072,768]{2,1,0:T(8,128)} %refs_0_.13, f32[3,3072,768]{2,1,0:T(8,128)} %refs_1_.13, ...), custom_call_target="tpu_custom_call", output_to_operand_aliasing={{0}: (8, {}), {1}: (9, {}), {2}: (10, {})} | custom-call | flops 2123366400 | bytes 66060288 | tf_op jit(solution)/shard_map/pallas_call | solution.py:321
  853.1 28.1 %shard_map.221 = (f32[3,768,3072]{2,1,0:T(8,128)}, f32[3,768,3072]{2,1,0:T(8,128)}, f32[3,768,3072]{2,1,0:T(8,128)}, bf16[768,3072]{1,0:T(8,128)(2,1)}) custom-call(s32[1]{0:T(128)} %bitcast.i_ref, f32[3,768,3072]{2,1,0:T(8,128)} %refs_0_.10, f32[3,768,3072]{2,1,0:T(8,128)} %refs_1_.10, ...), custom_call_target="tpu_custom_call", output_to_operand_aliasing={{0}: (8, {}), {1}: (9, {}), {2}: (10, {})} | custom-call | flops 2123366400 | bytes 66060288 | tf_op jit(solution)/shard_map/pallas_call | solution.py:321
  881.2 69.5 %forward.1 = f32[2048,768]{1,0:T(8,128)} custom-call(f32[2048,768]{1,0:T(8,128)} %shard_map.225.h_ref, bf16[768,3072]{1,0:T(8,128)(2,1)} %get-tuple-element.107.refs_0_, bf16[768,3072]{1,0:T(8,128)(2,1)} %get-tuple-element.108.refs_1_, bf16[768,3072]{1,0:T(8,128)(2,1)} %get-tuple-element.109.refs_2_, bf16[3072,768]{1,0:T(8,128)(2,1)} %get-tuple-element.110.refs_3_, ...), custom_call_target="tpu_custom_call" | custom-call | flops 57982058496 | bytes 40894464 | tf_op jit(solution)/shard_map/forward/pallas_call | solution.py:385
  950.8 4.6 multiply_reduce_fusion
  955.4 0.6 broadcast_multiply_fusion
  (26 shorter events, 0.1 us)
Async XLA Ops:
  27.6 207.4 %collective-permute-start.3 = (f32[2048,768]{1,0:T(8,128)}, f32[2048,768]{1,0:T(8,128)}, u32[]{:S(2)}, u32[]{:S(2)}) collective-permute-start(f32[2048,768]{1,0:T(8,128)} %shard_map.212.h_ref), channel_id=1, source_target_pairs={{0,2},{2,0},{1,3},{3,1},{4,6},{6,4},{5,7},{7,5}} | collective-permute-start | bytes 18874376 | tf_op jit(solution)/shard_map/ppermute | solution.py:416
  30.9 204.1 %collective-permute-start.4 = (bf16[2048,768]{1,0:T(8,128)(2,1)}, bf16[2048,768]{1,0:T(8,128)(2,1)}, u32[]{:S(2)}, u32[]{:S(2)}) collective-permute-start(bf16[2048,768]{1,0:T(8,128)(2,1)} %y_ref.1), channel_id=1, source_target_pairs={{0,2},{2,0},{1,3},{3,1},{4,6},{6,4},{5,7},{7,5}} | collective-permute-start | bytes 9437192 | tf_op jit(solution)/shard_map/ppermute | solution.py:416
  30.9 22.3 %copy-start = (f32[3,3072,768]{2,1,0:T(8,128)S(1)}, f32[3,3072,768]{2,1,0:T(8,128)}, u32[]{:S(2)}) copy-start(f32[3,3072,768]{2,1,0:T(8,128)} %refs_0_.13) | copy-start | bytes 84934656
  228.6 148.3 %collective-permute-start = (bf16[768,1536]{1,0:T(8,128)(2,1)}, bf16[768,1536]{1,0:T(8,128)(2,1)}, u32[]{:S(2)}, u32[]{:S(2)}) collective-permute-start(bf16[768,1536]{1,0:T(8,128)(2,1)} %get-tuple-element.64), channel_id=1, source_target_pairs={{0,1},{1,0},{2,3},{3,2},{4,5},{5,4},{6,7},{7,6}} | collective-permute-start | bytes 7077896 | tf_op jit(solution)/shard_map/ppermute | solution.py:416
  228.6 148.3 %collective-permute-start.1 = (bf16[768,1536]{1,0:T(8,128)(2,1)}, bf16[768,1536]{1,0:T(8,128)(2,1)}, u32[]{:S(2)}, u32[]{:S(2)}) collective-permute-start(bf16[768,1536]{1,0:T(8,128)(2,1)} %get-tuple-element.65), channel_id=1, source_target_pairs={{0,2},{2,0},{1,3},{3,1},{4,6},{6,4},{5,7},{7,5}} | collective-permute-start | bytes 7077896 | tf_op jit(solution)/shard_map/ppermute | solution.py:416
  230.6 146.4 %collective-permute-start.2 = (bf16[768,1536]{1,0:T(8,128)(2,1)}, bf16[768,1536]{1,0:T(8,128)(2,1)}, u32[]{:S(2)}, u32[]{:S(2)}) collective-permute-start(bf16[768,1536]{1,0:T(8,128)(2,1)} %get-tuple-element.66), channel_id=1, source_target_pairs={{0,3},{3,0},{1,2},{2,1},{4,7},{7,4},{5,6},{6,5}} | collective-permute-start | bytes 7077896 | tf_op jit(solution)/shard_map/ppermute | solution.py:416
  411.8 29.0 %collective-permute-start.8 = (f32[4,768,768]{2,1,0:T(8,128)}, f32[4,768,768]{2,1,0:T(8,128)}, u32[]{:S(2)}, u32[]{:S(2)}) collective-permute-start(f32[4,768,768]{2,1,0:T(8,128)} %shard_map.216), channel_id=1, source_target_pairs={{0,1},{1,0},{2,3},{3,2},{4,5},{5,4},{6,7},{7,6}} | collective-permute-start | bytes 28311560 | tf_op jit(solution)/shard_map/ppermute | solution.py:416
  440.3 91.1 %collective-permute-start.13 = (f32[4,768,768]{2,1,0:T(8,128)}, f32[4,768,768]{2,1,0:T(8,128)}, u32[]{:S(2)}, u32[]{:S(2)}) collective-permute-start(f32[4,768,768]{2,1,0:T(8,128)} %shard_map.218), channel_id=1, source_target_pairs={{0,1},{1,0},{2,3},{3,2},{4,5},{5,4},{6,7},{7,6}} | collective-permute-start | bytes 28311560 | tf_op jit(solution)/shard_map/ppermute | solution.py:416
  475.4 62.4 %copy-start.1 = (f32[4,768,768]{2,1,0:T(8,128)S(1)}, f32[4,768,768]{2,1,0:T(8,128)}, u32[]{:S(2)}) copy-start(f32[4,768,768]{2,1,0:T(8,128)} %shard_map.217) | copy-start | bytes 28311556
  475.5 61.8 %collective-permute-start.9 = (f32[4,768,768]{2,1,0:T(8,128)}, f32[4,768,768]{2,1,0:T(8,128)S(1)}, u32[]{:S(2)}, u32[]{:S(2)}) collective-permute-start(f32[4,768,768]{2,1,0:T(8,128)} %shard_map.217), channel_id=1, source_target_pairs={{0,1},{1,0},{2,3},{3,2},{4,5},{5,4},{6,7},{7,6}} | collective-permute-start | bytes 28311560 | tf_op jit(solution)/shard_map/ppermute | solution.py:416
  475.5 54.1 %collective-permute-start.6 = (bf16[768,1536]{1,0:T(8,128)(2,1)}, bf16[768,1536]{1,0:T(8,128)(2,1)S(1)}, u32[]{:S(2)}, u32[]{:S(2)}) collective-permute-start(bf16[768,1536]{1,0:T(8,128)(2,1)} %add_convert_fusion.refs_3_), channel_id=1, source_target_pairs={{0,2},{2,0},{1,3},{3,1},{4,6},{6,4},{5,7},{7,5}} | collective-permute-start | bytes 7077896 | tf_op jit(solution)/shard_map/ppermute | solution.py:416
  477.5 62.2 %collective-permute-start.5 = (bf16[768,1536]{1,0:T(8,128)(2,1)}, bf16[768,1536]{1,0:T(8,128)(2,1)S(1)}, u32[]{:S(2)}, u32[]{:S(2)}) collective-permute-start(bf16[768,1536]{1,0:T(8,128)(2,1)} %add_convert_fusion.refs_3_), channel_id=1, source_target_pairs={{0,1},{1,0},{2,3},{3,2},{4,5},{5,4},{6,7},{7,6}} | collective-permute-start | bytes 7077896 | tf_op jit(solution)/shard_map/ppermute | solution.py:416
  529.6 10.1 %copy-start.2 = (bf16[768,1536]{1,0:T(8,128)(2,1)}, bf16[768,1536]{1,0:T(8,128)(2,1)S(1)}, u32[]{:S(2)}) copy-start(bf16[768,1536]{1,0:T(8,128)(2,1)S(1)} %collective-permute-done.6.refs_5_) | copy-start | bytes 7077892
  529.6 54.4 %collective-permute-start.7 = (bf16[768,1536]{1,0:T(8,128)(2,1)S(1)}, bf16[768,1536]{1,0:T(8,128)(2,1)S(1)}, u32[]{:S(2)}, u32[]{:S(2)}) collective-permute-start(bf16[768,1536]{1,0:T(8,128)(2,1)S(1)} %collective-permute-done.6.refs_5_), channel_id=1, source_target_pairs={{0,1},{1,0},{2,3},{3,2},{4,5},{5,4},{6,7},{7,6}} | collective-permute-start | bytes 7077896 | tf_op jit(solution)/shard_map/ppermute | solution.py:416
  529.6 54.4 %collective-permute-start.18 = (bf16[2,768,768]{2,1,0:T(8,128)(2,1)}, bf16[2,768,768]{2,1,0:T(8,128)(2,1)}, u32[]{:S(2)}, u32[]{:S(2)}) collective-permute-start(bf16[2,768,768]{2,1,0:T(8,128)(2,1)} %fusion.2.refs_3_), channel_id=1, source_target_pairs={{0,2},{2,0},{1,3},{3,1},{4,6},{6,4},{5,7},{7,5}} | collective-permute-start | bytes 7077896 | tf_op jit(solution)/shard_map/ppermute | solution.py:416
  531.4 156.1 %collective-permute-start.17 = (bf16[2,768,768]{2,1,0:T(8,128)(2,1)}, bf16[2,768,768]{2,1,0:T(8,128)(2,1)}, u32[]{:S(2)}, u32[]{:S(2)}) collective-permute-start(bf16[2,768,768]{2,1,0:T(8,128)(2,1)} %fusion.2.refs_3_), channel_id=1, source_target_pairs={{0,1},{1,0},{2,3},{3,2},{4,5},{5,4},{6,7},{7,6}} | collective-permute-start | bytes 7077896 | tf_op jit(solution)/shard_map/ppermute | solution.py:416
  537.3 97.3 %collective-permute-start.15 = (bf16[2,768,768]{2,1,0:T(8,128)(2,1)}, bf16[2,768,768]{2,1,0:T(8,128)(2,1)}, u32[]{:S(2)}, u32[]{:S(2)}) collective-permute-start(bf16[2,768,768]{2,1,0:T(8,128)(2,1)} %fusion.refs_3_), channel_id=1, source_target_pairs={{0,2},{2,0},{1,3},{3,1},{4,6},{6,4},{5,7},{7,5}} | collective-permute-start | bytes 7077896 | tf_op jit(solution)/shard_map/ppermute | solution.py:416
  539.7 44.3 %copy-start.3 = (bf16[768,1536]{1,0:T(8,128)(2,1)}, bf16[768,1536]{1,0:T(8,128)(2,1)S(1)}, u32[]{:S(2)}) copy-start(bf16[768,1536]{1,0:T(8,128)(2,1)S(1)} %collective-permute-done.5.refs_4_) | copy-start | bytes 7077892
  539.7 148.1 %collective-permute-start.11 = (bf16[2,768,768]{2,1,0:T(8,128)(2,1)}, bf16[2,768,768]{2,1,0:T(8,128)(2,1)}, u32[]{:S(2)}, u32[]{:S(2)}) collective-permute-start(bf16[2,768,768]{2,1,0:T(8,128)(2,1)} %fusion.1.refs_3_), channel_id=1, source_target_pairs={{0,2},{2,0},{1,3},{3,1},{4,6},{6,4},{5,7},{7,5}} | collective-permute-start | bytes 7077896 | tf_op jit(solution)/shard_map/ppermute | solution.py:416
  584.0 130.4 %collective-permute-start.19 = (bf16[2,768,768]{2,1,0:T(8,128)(2,1)}, bf16[2,768,768]{2,1,0:T(8,128)(2,1)}, u32[]{:S(2)}, u32[]{:S(2)}) collective-permute-start(bf16[2,768,768]{2,1,0:T(8,128)(2,1)} %collective-permute-done.18.refs_5_), channel_id=1, source_target_pairs={{0,1},{1,0},{2,3},{3,2},{4,5},{5,4},{6,7},{7,6}} | collective-permute-start | bytes 7077896 | tf_op jit(solution)/shard_map/ppermute | solution.py:416
  584.1 1.4 copy-start.4
  584.1 185.9 %collective-permute-start.14 = (bf16[2,768,768]{2,1,0:T(8,128)(2,1)}, bf16[2,768,768]{2,1,0:T(8,128)(2,1)}, u32[]{:S(2)}, u32[]{:S(2)}) collective-permute-start(bf16[2,768,768]{2,1,0:T(8,128)(2,1)} %fusion.refs_3_), channel_id=1, source_target_pairs={{0,1},{1,0},{2,3},{3,2},{4,5},{5,4},{6,7},{7,6}} | collective-permute-start | bytes 7077896 | tf_op jit(solution)/shard_map/ppermute | solution.py:416
  634.6 135.4 %collective-permute-start.16 = (bf16[2,768,768]{2,1,0:T(8,128)(2,1)}, bf16[2,768,768]{2,1,0:T(8,128)(2,1)}, u32[]{:S(2)}, u32[]{:S(2)}) collective-permute-start(bf16[2,768,768]{2,1,0:T(8,128)(2,1)} %collective-permute-done.15.refs_5_), channel_id=1, source_target_pairs={{0,1},{1,0},{2,3},{3,2},{4,5},{5,4},{6,7},{7,6}} | collective-permute-start | bytes 7077896 | tf_op jit(solution)/shard_map/ppermute | solution.py:416
  687.5 138.0 %collective-permute-start.10 = (bf16[2,768,768]{2,1,0:T(8,128)(2,1)}, bf16[2,768,768]{2,1,0:T(8,128)(2,1)}, u32[]{:S(2)}, u32[]{:S(2)}) collective-permute-start(bf16[2,768,768]{2,1,0:T(8,128)(2,1)} %fusion.1.refs_3_), channel_id=1, source_target_pairs={{0,1},{1,0},{2,3},{3,2},{4,5},{5,4},{6,7},{7,6}} | collective-permute-start | bytes 7077896 | tf_op jit(solution)/shard_map/ppermute | solution.py:416
  687.8 137.7 %collective-permute-start.12 = (bf16[2,768,768]{2,1,0:T(8,128)(2,1)}, bf16[2,768,768]{2,1,0:T(8,128)(2,1)}, u32[]{:S(2)}, u32[]{:S(2)}) collective-permute-start(bf16[2,768,768]{2,1,0:T(8,128)(2,1)} %collective-permute-done.11.refs_5_), channel_id=1, source_target_pairs={{0,1},{1,0},{2,3},{3,2},{4,5},{5,4},{6,7},{7,6}} | collective-permute-start | bytes 7077896 | tf_op jit(solution)/shard_map/ppermute | solution.py:416

commit v3 on v2

v3 whole, which is shorter than its diff:
```python
import functools

import jax
import jax.numpy as jnp
from jax import lax
from jax.experimental import pallas as pl
from jax.experimental.pallas import tpu as pltpu
from jax.sharding import PartitionSpec as P


BETA1 = 0.9
BETA2 = 0.999
BC1 = 1.0 / (1.0 - BETA1 ** 10)
BC2 = 1.0 / (1.0 - BETA2 ** 10)
EPS = 1e-12
WD = 0.01
ETA = 0.05
R2 = 0.7071067811865476
R2PI = 0.3989422804014327
BF = jnp.bfloat16
F32 = jnp.float32
VMEM = 67043328
ANY = pl.BlockSpec(memory_space=pl.ANY)

D2D = [(0, 1), (1, 0), (2, 3), (3, 2)]
CROSS = [(0, 2), (2, 0), (1, 3), (3, 1)]
DIAG = [(0, 3), (3, 0), (1, 2), (2, 1)]


def dot(a, b):
    return jnp.dot(a, b, preferred_element_type=F32)


def dot_nt(a, b):
    return lax.dot_general(a, b, (((1,), (1,)), ((), ())), preferred_element_type=F32)


def gelu(a):
    return (0.5 * a) * (1.0 + lax.erf(a * R2))


def gelu_grad(a):
    return 0.5 * (1.0 + lax.erf(a * R2)) + a * jnp.exp(-0.5 * a * a) * R2PI


def params(*sem):
    return pltpu.CompilerParams(vmem_limit_bytes=VMEM, dimension_semantics=sem)


def cost(flops, nbytes):
    return pl.CostEstimate(flops=int(flops), bytes_accessed=int(nbytes), transcendentals=0)


def in_kernel(x_ref, w_ref, o_ref):
    @pl.when(pl.program_id(0) == 0)
    def _():
        o_ref[...] = jnp.zeros_like(o_ref)

    o_ref[...] += dot(x_ref[...], w_ref[...].astype(BF))


def in_matmul(x, w, kb=768):
    t, e = x.shape
    d = w.shape[1]
    return pl.pallas_call(
        in_kernel,
        grid=(e // kb,),
        in_specs=[pl.BlockSpec((t, kb), lambda k: (0, k)), pl.BlockSpec((kb, d), lambda k: (k, 0))],
        out_specs=pl.BlockSpec((t, d), lambda k: (0, 0)),
        out_shape=jax.ShapeDtypeStruct((t, d), F32),
        compiler_params=params("arbitrary"),
        cost_estimate=cost(2 * t * e * d, 2 * t * e + w.nbytes + 4 * t * d),
    )(x, w)


def chain_kernel(scale, dev, nm, c_ref, h_ref, y_ref, w1_hbm, w2_hbm, *rest):
    t_o, p_o, g0_o, w1, w2, a_s, s_s, h_s, b_s, sem = rest[2 * (dev > 0):]
    t = pl.program_id(0)
    c = c_ref[0]
    nl, _, f = w1.shape
    half = f // 2
    fc = half // nm

    def copies(l):
        out = []
        for k in range(2):
            src = pl.multiple_of(lax.rem(c + k, 2) * half, half)
            out.append(pltpu.make_async_copy(w1_hbm.at[l, :, pl.ds(src, half)], w1.at[l, :, pl.ds(k * half, half)],
                                             sem.at[l, k]))
            out.append(pltpu.make_async_copy(w2_hbm.at[l, pl.ds(src, half), :], w2.at[l, pl.ds(k * half, half), :],
                                             sem.at[l, k + 2]))
        return out

    @pl.when(t == 0)
    def _():
        for l in range(nl):
            for cp in copies(l):
                cp.start()

    h_s[...] = h_ref[...]

    def fwd(l, carry):
        @pl.when(t == 0)
        def _():
            for cp in copies(l):
                cp.wait()

        b_s[...] = h_s[...].astype(BF)

        def up(j):
            a_s[l, :, j * fc:(j + 1) * fc] = dot(b_s[...], w1[l, :, j * fc:(j + 1) * fc])

        up(0)
        t_o[0, l, nm] = b_s[...].T
        for j in range(2 * nm):
            if j + 1 < 2 * nm:
                up(j + 1)
            s_s[:, j * fc:(j + 1) * fc] = gelu(a_s[l, :, j * fc:(j + 1) * fc]).astype(BF)
            h_s[...] += dot(s_s[:, j * fc:(j + 1) * fc], w2[l, j * fc:(j + 1) * fc, :])
            if j < nm:
                t_o[0, l, j] = s_s[:, j * fc:(j + 1) * fc].T
        return carry

    def bwd(k, carry):
        l = nl - 1 - k
        p_o[0, l, 0] = h_s[...].astype(BF)

        def down(j):
            return dot_nt(p_o[0, l, 0], w2[l, j * fc:(j + 1) * fc, :])

        def piece(j):
            return p_o.at[0, l, 1 + j] if j < nm else s_s.at[:, j * fc:(j + 1) * fc]

        de = down(0)
        for j in range(2 * nm):
            nxt = down(j + 1) if j + 1 < 2 * nm else None
            piece(j)[...] = (de * gelu_grad(a_s[l, :, j * fc:(j + 1) * fc])).astype(BF)
            h_s[...] += dot_nt(piece(j)[...], w1[l, :, j * fc:(j + 1) * fc])
            de = nxt
        return carry

    lax.fori_loop(0, nl, fwd, 0)
    h_s[...] = (h_s[...] - y_ref[...].astype(F32)) * scale
    lax.fori_loop(0, nl, bwd, 0)
    g0_o[...] = h_s[...].astype(BF).T


def chain(c, h, y, w1, w2, scale, prev=None, tm=256, nm=2):
    t, d = h.shape
    nl, _, f = w1.shape
    dev = 0 if prev is None else 1
    tok = pl.BlockSpec((tm, d), lambda i, c: (i, 0))
    return pl.pallas_call(
        functools.partial(chain_kernel, scale, dev, nm),
        grid_spec=pltpu.PrefetchScalarGridSpec(
            num_scalar_prefetch=1,
            grid=(t // tm,),
            in_specs=[tok, tok, ANY, ANY] + [ANY] * (2 * dev),
            out_specs=[pl.BlockSpec((1, nl, nm + 1, d, tm), lambda i, c: (dev, 0, 0, 0, i)),
                       pl.BlockSpec((1, nl, nm + 1, tm, d), lambda i, c: (dev, 0, 0, i, 0)),
                       pl.BlockSpec((d, tm), lambda i, c: (0, i))],
            scratch_shapes=[
                pltpu.VMEM((nl, d, f), BF),
                pltpu.VMEM((nl, f, d), BF),
                pltpu.VMEM((nl, tm, f), F32),
                pltpu.VMEM((tm, f), BF),
                pltpu.VMEM((tm, d), F32),
                pltpu.VMEM((tm, d), BF),
                pltpu.SemaphoreType.DMA((nl, 4)),
            ],
        ),
        out_shape=[jax.ShapeDtypeStruct((2, nl, nm + 1, d, t), BF), jax.ShapeDtypeStruct((2, nl, nm + 1, t, d), BF),
                   jax.ShapeDtypeStruct((d, t), BF)],
        input_output_aliases={5 + k: k for k in range(2 * dev)},
        compiler_params=params("arbitrary"),
        cost_estimate=cost(8 * nl * t * d * f, 4 * nl * d * f + 8 * t * d + 4 * nl * t * 3 * d),
    )(c, h, y, w1, w2, *(prev or ()))


def dw_kernel(i_ref, t_ref, p_ref, o_ref):
    r = dot(t_ref[0, 0, 0], p_ref[0, 0, 0]).astype(BF).astype(F32)
    o_ref[0] = jnp.where(pl.program_id(1) == 0, 0.0, o_ref[0]) + r


def dw_half(core, acts, l):
    ts, ps = acts
    d, t = ts.shape[3:]

    def quarter(job, c):
        return jnp.where(job < 2, 1 - c[0], c[0])

    def tplane(job, dev, c):
        return (dev, l, jnp.where(job % 2 == 0, quarter(job, c), 2), 0, 0)

    def pplane(job, dev, c):
        return (dev, l, jnp.where(job % 2 == 0, 0, quarter(job, c) + 1), 0, 0)

    return pl.pallas_call(
        dw_kernel,
        grid_spec=pltpu.PrefetchScalarGridSpec(
            num_scalar_prefetch=1,
            grid=(4, 2),
            in_specs=[pl.BlockSpec((1, 1, 1, d, t), tplane), pl.BlockSpec((1, 1, 1, t, d), pplane)],
            out_specs=pl.BlockSpec((1, d, d), lambda job, dev, c: (job, 0, 0)),
        ),
        out_shape=jax.ShapeDtypeStruct((4, d, d), F32),
        compiler_params=params("arbitrary", "arbitrary"),
        cost_estimate=cost(16 * t * d * d, 32 * t * d + 16 * d * d),
    )(core, ts, ps)


def dwi_kernel(i_ref, g_ref, x_ref, *refs):
    acc = refs[-1]
    acc[...] = dot(g_ref[...], x_ref[...]).T
    for k in range(4):
        @pl.when(pl.program_id(0) == k)
        def _(k=k):
            refs[k][...] = acc[...].astype(BF)


def dwi_quarters(i, g, x, eb=512):
    t, e = x.shape
    d = g.shape[0]
    n = e // 4 // eb

    def quarter(k, i):
        return jnp.bitwise_xor(jnp.where(k == 0, 2, jnp.where(k == 1, 3, jnp.where(k == 2, 1, 0))), i[0])

    def at(kk):
        return lambda k, j, i: (jnp.where(k < kk, 0, jnp.where(k > kk, n - 1, j)), 0)

    return pl.pallas_call(
        dwi_kernel,
        grid_spec=pltpu.PrefetchScalarGridSpec(
            num_scalar_prefetch=1,
            grid=(4, n),
            in_specs=[pl.BlockSpec((d, t), lambda k, j, i: (0, 0)),
                      pl.BlockSpec((t, eb), lambda k, j, i: (0, quarter(k, i) * n + j))],
            out_specs=[pl.BlockSpec((eb, d), at(kk)) for kk in range(4)],
            scratch_shapes=[pltpu.VMEM((eb, d), F32)],
        ),
        out_shape=[jax.ShapeDtypeStruct((e // 4, d), BF)] * 4,
        compiler_params=params("arbitrary", "arbitrary"),
        cost_estimate=cost(2 * t * e * d, 2 * t * (e + d) + 2 * d * e),
        name="dwi",
    )(i, g, x)


RB = 192
STRIP = 16
RING = 6
AHEAD = 3


class Forward:
    TM = 256

    def __init__(self, h, w1, w2):
        self.args = (h, w1, w2)
        self.t, self.d = h.shape
        self.nc, _, self.fc = w1.shape
        self.units = self.t // self.TM * self.nc
        self.flops = 4 * self.t * self.d * self.nc * self.fc
        nt = self.t // self.TM
        self.scratch = [
            pltpu.VMEM(w1.shape, BF),
            pltpu.VMEM(w2.shape, BF),
            pltpu.VMEM((nt, self.TM, self.d), F32),
            pltpu.VMEM((self.TM, self.d), BF),
            pltpu.VMEM((self.TM, self.fc), F32),
            pltpu.VMEM((self.TM, self.fc), BF),
            pltpu.SemaphoreType.DMA((self.nc,)),
            pltpu.SemaphoreType.DMA((nt,)),
        ]

    def bind(self, ins, out, scratch):
        self.h, self.w1, self.w2 = ins
        self.out = out
        self.w1_s, self.w2_s, self.h_s, self.b_s, self.a_s, self.s_s, self.wsem, self.hsem = scratch

    def tile(self, t):
        return pltpu.make_async_copy(self.h.at[pl.ds(pl.multiple_of(t * self.TM, self.TM), self.TM)], self.h_s.at[t],
                                     self.hsem.at[t])

    def weights(self, c):
        return (pltpu.make_async_copy(self.w1.at[c], self.w1_s.at[c], self.wsem.at[c]),
                pltpu.make_async_copy(self.w2.at[c], self.w2_s.at[c], self.wsem.at[c]))

    def start(self):
        for c in range(self.nc):
            if c < self.t // self.TM:
                self.tile(c).start()
            for cp in self.weights(c):
                cp.start()
        for t in range(self.nc, self.t // self.TM):
            self.tile(t).start()
        self.s_s[...] = jnp.zeros_like(self.s_s)

    def before(self, n):
        @pl.when(n < self.nc)
        def _():
            for cp in self.weights(n):
                cp.wait()

        @pl.when(n % self.nc == 0)
        def _():
            t = n // self.nc
            self.tile(t).wait()
            self.b_s[...] = self.h_s[t].astype(BF)

    def down(self, n, n0):
        t, c = n // self.nc, n % self.nc
        self.h_s[t, :, n0:n0 + 256] += dot(self.s_s[...], self.w2_s[c, :, n0:n0 + 256])

    def work(self, n):
        last = jnp.maximum(n - 1, 0)
        c = n % self.nc

        def up(n0):
            self.a_s[:, n0:n0 + 256] = dot(self.b_s[...], self.w1_s[c, :, n0:n0 + 256])

        return ([functools.partial(self.down, last, n0) for n0 in range(0, self.d, 256)]
                + [functools.partial(up, n0) for n0 in range(0, self.fc, 256)])

    def after(self, n):
        for r in range(0, self.TM, STRIP):
            self.s_s[r:r + STRIP] = gelu(self.a_s[r:r + STRIP]).astype(BF)

    def finish(self):
        for n0 in range(0, self.d, 256):
            self.down(self.units - 1, n0)
        nt = self.t // self.TM
        out = [pltpu.make_async_copy(self.h_s.at[t], self.out.at[pl.ds(t * self.TM, self.TM)], self.hsem.at[t])
               for t in range(nt)]
        for cp in out:
            cp.start()
        return out


class Input:
    KB = 768
    XR = 4

    def __init__(self, x, w):
        self.args = (x, w)
        self.t, self.e = x.shape
        self.d = w.shape[-1]
        self.mb = self.t // 4
        self.units = 4 * self.e // self.KB
        self.flops = 2 * self.t * self.e * self.d
        self.scratch = [
            pltpu.VMEM((self.XR, self.mb, self.KB), BF),
            pltpu.VMEM((2, self.KB, self.d), BF),
            pltpu.VMEM((4, self.mb, self.d), F32),
            pltpu.SemaphoreType.DMA((self.XR,)),
            pltpu.SemaphoreType.DMA((2,)),
            pltpu.SemaphoreType.DMA((1,)),
        ]

    def bind(self, ins, out, scratch):
        self.x, self.w = ins
        self.out = out
        self.x_s, self.w_s, self.h_s, self.xsem, self.wsem, self.osem = scratch

    def xcopy(self, n):
        src = self.x.at[pl.ds(pl.multiple_of(n % 4 * self.mb, self.mb), self.mb),
                        pl.ds(pl.multiple_of(n // 4 * self.KB, self.KB), self.KB)]
        return pltpu.make_async_copy(src, self.x_s.at[n % self.XR], self.xsem.at[n % self.XR])

    def wcopy(self, k):
        return pltpu.make_async_copy(self.w.at[k], self.w_s.at[k % 2], self.wsem.at[k % 2])

    def start(self):
        self.wcopy(0).start()
        for n in range(self.XR - 1):
            self.xcopy(n).start()
        self.h_s[...] = jnp.zeros_like(self.h_s)

    def before(self, n):
        self.xcopy(n).wait()

        @pl.when(n + self.XR - 1 < self.units)
        def _():
            self.xcopy(n + self.XR - 1).start()

        @pl.when(n % 4 == 0)
        def _():
            self.wcopy(n // 4).wait()

            @pl.when(n + 4 < self.units)
            def _():
                self.wcopy(n // 4 + 1).start()

    def work(self, n):
        m, xr, wr = n % 4, n % self.XR, n // 4 % 2

        def part(n0):
            self.h_s[m, :, n0:n0 + 256] += dot(self.x_s[xr], self.w_s[wr, :, n0:n0 + 256])

        return [functools.partial(part, n0) for n0 in range(0, self.d, 256)]

    def after(self, n):
        pass

    def finish(self):
        out = [pltpu.make_async_copy(self.h_s.at[m], self.out.at[pl.ds(m * self.mb, self.mb)], self.osem.at[0])
               for m in range(4)]
        for cp in out:
            cp.start()
        return out


def lamb_kernel(mats, job, *refs):
    i_ref, refs = refs[0], list(refs[1:])

    def take(n):
        out = refs[:n]
        del refs[:n]
        return out

    nm = len(mats)
    state = [take(3) for _ in mats]
    pieces = take(4)
    ins = take(len(job.args)) if job else []
    take(sum(3 for mat in mats if mat[3]))
    outs = [take(3) for _ in mats]
    lows = take(nm)
    out = take(1)[0] if job else None
    w_s, u_s, mv, g_s, b_s, sw, su, ratio, isem, osem, wsem, bsem = take(12)
    if job:
        job.bind(ins, out, refs)
    i = i_ref[0]
    nq = mats[0][2]
    nb = 4 * nq
    width = w_s.shape[2]
    qrows = nq * RB

    def block(m, ref, b):
        l = mats[m][0]
        q = jnp.bitwise_xor(b // nq, i)
        r = b % nq * RB
        if l is None:
            return ref.at[pl.ds(pl.multiple_of(q * qrows + r, RB), RB)]
        if ref.shape[2] == width:
            return ref.at[l, pl.ds(pl.multiple_of(q * qrows + r, RB), RB)]
        return ref.at[l, pl.ds(pl.multiple_of(r, RB), RB), pl.ds(pl.multiple_of(q * width, width), width)]

    def loads(m, b, n):
        r = n % RING
        w, mm, v = state[m]
        return (pltpu.make_async_copy(block(m, w, b), w_s.at[b], isem.at[r]),
                pltpu.make_async_copy(block(m, mm, b), mv.at[r, 0], isem.at[r]),
                pltpu.make_async_copy(block(m, v, b), mv.at[r, 1], isem.at[r]))

    def piece(m, k, b, n):
        gi = mats[m][1]
        src = pieces[k] if gi is None else pieces[k].at[gi]
        r = n % RING
        return pltpu.make_async_copy(src.at[pl.ds(pl.multiple_of(b % nq * RB, RB), RB)], g_s.at[r], isem.at[r])

    def load(m, b, n):
        for cp in loads(m, b, n):
            cp.start()
        for k in range(4):
            @pl.when(b // nq == k)
            def _(k=k):
                piece(m, k, b, n).start()

    def stores(m, b, n):
        r = n % RING
        return (pltpu.make_async_copy(mv.at[r, 0], block(m, outs[m][1], b), osem.at[r]),
                pltpu.make_async_copy(mv.at[r, 1], block(m, outs[m][2], b), osem.at[r]))

    def new(m, b):
        return pltpu.make_async_copy(w_s.at[b], block(m, outs[m][0], b), wsem.at[b])

    def low(m, b):
        q = jnp.bitwise_xor(b // nq, i)
        row = pl.multiple_of(q * qrows + b % nq * RB, RB)
        return pltpu.make_async_copy(b_s.at[b], lows[m].at[pl.ds(row, RB)], bsem.at[0])

    def strip(b, r, r0, sums):
        sl = pl.ds(r0, STRIP)
        w = w_s[b, sl]
        g = g_s[r, sl].astype(F32)
        m2 = BETA1 * mv[r, 0, sl] + (1.0 - BETA1) * g
        v2 = BETA2 * mv[r, 1, sl] + (1.0 - BETA2) * g * g
        u = BC1 * m2 / (jnp.sqrt(BC2 * v2) + EPS) + WD * w
        mv[r, 0, sl] = m2
        mv[r, 1, sl] = v2
        u_s[b, sl] = u
        for k in range(0, STRIP, 8):
            sums[0] = sums[0] + w[k:k + 8] * w[k:k + 8]
            sums[1] = sums[1] + u[k:k + 8] * u[k:k + 8]

    for b in range(AHEAD):
        load(0, b, b)
    if job:
        job.start()

    for m in range(nm):
        base = m * nb
        if m:
            for b in range(AHEAD):
                new(m - 1, b).wait()
                load(m, b, base + b)
        sw[...] = jnp.zeros_like(sw)
        su[...] = jnp.zeros_like(su)

        def sweep(b, carry):
            n = base + b
            r = n % RING
            for cp in loads(m, b, n):
                cp.wait()
            piece(m, 0, b, n).wait()

            @pl.when(n >= RING - AHEAD)
            def _():
                for cp in stores(m, b, n - (RING - AHEAD)):
                    cp.wait()

            @pl.when(b + AHEAD < nb)
            def _():
                if m:
                    new(m - 1, b + AHEAD).wait()
                load(m, b + AHEAD, n + AHEAD)

            sums = [jnp.zeros(sw.shape, F32), jnp.zeros(su.shape, F32)]
            if job:
                job.before(n)
            tasks = job.work(n) if job else []
            strips = list(range(0, RB, STRIP))
            per = -(-len(strips) // max(1, len(tasks)))
            for task in tasks:
                task()
                for r0 in strips[:per]:
                    strip(b, r, r0, sums)
                del strips[:per]
            for r0 in strips:
                strip(b, r, r0, sums)
            if job:
                job.after(n)
            sw[...] += sums[0]
            su[...] += sums[1]
            for cp in stores(m, b, n):
                cp.start()
            return carry

        lax.fori_loop(0, nb, sweep, 0)
        ratio[0] = ETA * (jnp.sqrt(jnp.sum(sw[...])) / jnp.sqrt(jnp.sum(su[...])))
        if job and m == nm - 1:
            flying = job.finish()

        def update(b, carry):
            if m:
                low(m - 1, b).wait()
            rt = ratio[0]
            for r0 in range(0, RB, STRIP):
                sl = pl.ds(r0, STRIP)
                w = w_s[b, sl] - rt * u_s[b, sl]
                w_s[b, sl] = w
                b_s[b, sl] = w.astype(BF)
            new(m, b).start()
            low(m, b).start()
            return carry

        lax.fori_loop(0, nb, update, 0)

    def drain(b, carry):
        new(nm - 1, b).wait()
        low(nm - 1, b).wait()
        return carry

    lax.fori_loop(0, nb, drain, 0)
    for n in range(nm * nb - (RING - AHEAD), nm * nb):
        for cp in stores(nm - 1, 0, n):
            cp.wait()
    if job:
        for cp in flying:
            cp.wait()


def lamb(i, mats, pieces, job=None):
    width = pieces[0].shape[-1]
    nq = pieces[0].shape[-2] // RB
    nb = 4 * nq
    args, outs, lows, bufs, aliases = [], [], [], [], {}
    for w, m, v, l, gi, old in mats:
        args += [w, m, v]
        outs += [jax.ShapeDtypeStruct(w.shape, F32)] * 3
        lows.append(jax.ShapeDtypeStruct((nb * RB, width), BF))
    args += pieces
    if job:
        args += job.args
    for k, mat in enumerate(mats):
        if mat[5] is not None:
            for c in range(3):
                aliases[1 + len(args) + len(bufs)] = 3 * k + c
                bufs.append(mat[5][c])
    size = nb * RB * width * len(mats)
    res = pl.pallas_call(
        functools.partial(lamb_kernel, [(l, gi, nq, old is not None) for _, _, _, l, gi, old in mats], job),
        in_specs=[pl.BlockSpec(memory_space=pltpu.SMEM)] + [ANY] * (len(args) + len(bufs)),
        out_specs=[ANY] * (len(outs) + len(lows) + bool(job)),
        out_shape=outs + lows + ([jax.ShapeDtypeStruct((job.t, job.d), F32)] if job else []),
        scratch_shapes=[
            pltpu.VMEM((nb, RB, width), F32),
            pltpu.VMEM((nb, RB, width), F32),
            pltpu.VMEM((RING, 2, RB, width), F32),
            pltpu.VMEM((RING, RB, width), BF),
            pltpu.VMEM((nb, RB, width), BF),
            pltpu.VMEM((8, width), F32),
            pltpu.VMEM((8, width), F32),
            pltpu.SMEM((1,), F32),
            pltpu.SemaphoreType.DMA((RING,)),
            pltpu.SemaphoreType.DMA((RING,)),
            pltpu.SemaphoreType.DMA((nb,)),
            pltpu.SemaphoreType.DMA((1,)),
        ] + (job.scratch if job else []),
        input_output_aliases=aliases,
        compiler_params=params(),
        cost_estimate=cost(1200 * size, 28 * size),
    )(i, *args, *bufs)
    n = len(mats)
    return [(res[3 * k:3 * k + 3], res[3 * n + k]) for k in range(n)], res[4 * n] if job else None


def last_kernel(h_ref, w1_hbm, w2_hbm, o_ref, w1, w2, a_s, s_s, b_s, sem):
    t = pl.program_id(0)
    nc = w1.shape[0]
    fc = w1.shape[2]

    def copies(c):
        return (pltpu.make_async_copy(w1_hbm.at[c], w1.at[c], sem.at[0, c]),
                pltpu.make_async_copy(w2_hbm.at[c], w2.at[c], sem.at[1, c]))

    @pl.when(t == 0)
    def _():
        for c in range(nc):
            for cp in copies(c):
                cp.start()
        for c in range(nc):
            for cp in copies(c):
                cp.wait()

    o_ref[...] = h_ref[...]
    b_s[...] = h_ref[...].astype(BF)

    def up(c):
        a_s[:, c * fc:(c + 1) * fc] = dot(b_s[...], w1[c])

    up(0)
    for c in range(nc):
        if c + 1 < nc:
            up(c + 1)
        s_s[:, c * fc:(c + 1) * fc] = gelu(a_s[:, c * fc:(c + 1) * fc]).astype(BF)
        o_ref[...] += dot(s_s[:, c * fc:(c + 1) * fc], w2[c])


def last_block(h, w1, w2, tm=256):
    t, d = h.shape
    nc, _, fc = w1.shape
    tok = pl.BlockSpec((tm, d), lambda i: (i, 0))
    return pl.pallas_call(
        last_kernel,
        grid=(t // tm,),
        in_specs=[tok, ANY, ANY],
        out_specs=tok,
        out_shape=jax.ShapeDtypeStruct((t, d), F32),
        scratch_shapes=[
            pltpu.VMEM(w1.shape, BF),
            pltpu.VMEM(w2.shape, BF),
            pltpu.VMEM((tm, nc * fc), F32),
            pltpu.VMEM((tm, nc * fc), BF),
            pltpu.VMEM((tm, d), BF),
            pltpu.SemaphoreType.DMA((2, nc)),
        ],
        compiler_params=params("arbitrary"),
        cost_estimate=cost(4 * t * d * nc * fc, 4 * d * nc * fc + 8 * t * d),
        name="last",
    )(h, w1, w2)


def solution(mesh):
    p = mesh.shape['data']

    def inner(wi, w1, w2, mi, vi, m1, v1, m2, v2, x0, y0, x1, y1):
        nl, d, _ = w1.shape
        scale = 1.0 / (x0.shape[0] * p * d)
        i = lax.axis_index('data').astype(jnp.int32)
        me = jnp.reshape(i, (1,))
        chip = me // 2
        core = me % 2

        def send(x, perm):
            return lax.ppermute(x, 'data', perm)

        def gather(g):
            far = send(g, CROSS)
            return g, send(g, D2D), far, send(far, D2D)

        y0o = send(y0, CROSS)
        h0 = in_matmul(x0, wi)
        h0o = send(h0, CROSS)
        w1b, w2b = w1.astype(BF), w2.astype(BF)
        *acts, g0 = chain(chip, h0, y0, w1b, w2b, scale)
        *far, near, own = dwi_quarters(me, g0, x0)
        got = [own, send(near, D2D), send(far[0], CROSS), send(far[1], DIAG)]
        *acts, _ = chain(chip, h0o, y0o, w1b, w2b, scale, lax.optimization_barrier((acts, own))[0])
        got, acts = lax.optimization_barrier((got, acts))
        si = sum(g.astype(F32) for g in got).astype(BF)
        gi = gather(si)
        gl = []
        for l in range(nl):
            acts = lax.optimization_barrier((acts, si if l == 0 else parts if l == 1 else gl[-1][0]))[0]
            last = parts if l else None
            parts = dw_half(core, acts, l)
            if l:
                gl.append(gather((last[2:] + other[:2]).astype(BF)))
            other = send(parts, D2D)
        gl.append(gather((parts[2:] + other[:2]).astype(BF)))
        [((wi_n, mi_n, vi_n), wib)], _ = lamb(me, [(wi, mi, vi, None, None, None)], gi)
        b1 = b2 = None
        h1 = None
        for l in range(nl):
            job = Input(x1, wib.reshape(-1, d, d)) if l == 0 else Forward(h1, wb1, wb2)
            [(b1, wb1), (b2, wb2)], h1 = lamb(me, [(w1, m1, v1, l, 1, b1), (w2, m2, v2, l, 0, b2)], gl[l], job)
            wb1, wb2 = wb1.reshape(-1, d, d), wb2.reshape(-1, d, d)
        h1 = last_block(h1, wb1, wb2)
        loss = jnp.sum((h1 - y1.astype(F32)) ** 2, axis=-1) / (2.0 * d)
        return (wi_n, b1[0], b2[0], mi_n, vi_n, b1[1], b1[2], b2[1], b2[2], loss, h1)

    w2s = P('rep', None)
    w3s = P('rep', None, None)
    ts = P(('rep', 'data'), None)
    return jax.shard_map(inner, mesh=mesh,
                         in_specs=(w2s, w3s, w3s, w2s, w2s, w3s, w3s, w3s, w3s, ts, ts, ts, ts),
                         out_specs=(w2s, w3s, w3s, w2s, w2s, w3s, w3s, w3s, w3s, P(('rep', 'data')), ts),
                         check_vma=False)
```

time: 964 us -> 953 us (0.989)
  Pallas kernels: 740 us -> 687 us
  waiting for transfers between devices: 148 us -> 192 us
    ppermute x20, waiting for transfers between devices: 148 us -> 192 us  [send(): return lax.ppermute(x, 'data', perm)]
    pallas_call x8 -> x5, Pallas kernels: 289 us -> 260 us  [the longest x4 233 us: lamb(): pl.pallas_call(functools.partial(lamb_kernel, [(l, gi, nq, old is not Non...]
    pallas_call x2 -> x1, Pallas kernels: 53.3 us -> 26.9 us  [in_matmul(): pl.pallas_call(in_kernel, grid=(e // kb,), in_specs=[pl.BlockSpec((t, kb)...]
  transfers between devices with their start and end apart: 20 -> 20, of which waited for: 4 -> 4; matrix products, arithmetic and copies ran while one was open for 4% -> 4% of each run, Pallas kernels for 58% -> 60%
where the time goes in v3:
time: 953 us; the launch traced here: 945 us
  Pallas kernels  687 us (72%)
  waiting for transfers between devices  192 us (20%)
  other arithmetic  47.7 us (5%)
  starting transfers between devices  11.3 us (1%)
    pallas_call x2, Pallas kernels, chain(): pl.pallas_call(functools.partial(chain_kernel, scale, dev, nm), grid_spec...  283 us
    pallas_call x4, Pallas kernels, lamb(): pl.pallas_call(functools.partial(lamb_kernel, [(l, gi, nq, old is not Non...  233 us
    ppermute x20, waiting for transfers between devices, send(): return lax.ppermute(x, 'data', perm)  192 us
    pallas_call x3, Pallas kernels, dw_half(): pl.pallas_call(dw_kernel, grid_spec=pltpu.PrefetchScalarGridSpec(num_scal...  85.6 us
    pallas_call x1, Pallas kernels, dwi_quarters(): pl.pallas_call(dwi_kernel, grid_spec=pltpu.PrefetchScalarGridSpec(num_sca...  31.1 us
    pallas_call x1, Pallas kernels, last_block(): pl.pallas_call(last_kernel, grid=(t // tm,), in_specs=[tok, ANY, ANY], ou...  27 us
    pallas_call x1, Pallas kernels, in_matmul(): pl.pallas_call(in_kernel, grid=(e // kb,), in_specs=[pl.BlockSpec((t, kb)...  26.9 us
    convert_element_type x2, other arithmetic, inner(): w1b, w2b = (w1.astype(BF), w2.astype(BF))  22.2 us
  transfers between devices with their start and end apart: 20, of which 4 were waited for; matrix products, arithmetic and copies ran while one was open for 4% of the time, Pallas kernels for 60%

profile of v3, /device:TPU:0, one launch (start us, length us, event | category | flops | bytes accessed | tf_op | source)
XLA Modules:
  0.0 945.0 jit_solution(3816349569369923703)
XLA Ops:
  0.6 3.3 collective-permute-start.4
  4.0 26.9 %shard_map.212.h_ref = f32[2048,768]{1,0:T(8,128)} custom-call(bf16[2048,6144]{1,0:T(8,128)(2,1)} %x_ref.3, f32[6144,768]{1,0:T(8,128)} %refs_1_.4), custom_call_target="tpu_custom_call" | custom-call | flops 19327352832 | bytes 50331648 | tf_op jit(solution)/shard_map/pallas_call | solution.py:65
  30.9 0.0 collective-permute-start.3
  30.9 16.2 %convert_element_type.33.w1_hbm = bf16[3,768,3072]{2,1,0:T(8,128)(2,1)} convert(f32[3,768,3072]{2,1,0:T(8,128)} %refs_1_.7) | non-fusion elementwise | flops 7077888 | bytes 42467328 | tf_op jit(solution)/shard_map/convert_element_type | solution.py:705
  47.1 6.1 copy-done
  53.2 6.0 convert_element_type.34.w2_hbm
  59.2 141.3 %shard_map.213 = (bf16[2,3,3,768,2048]{4,3,2,1,0:T(8,128)(2,1)}, bf16[2,3,3,2048,768]{4,3,2,1,0:T(8,128)(2,1)}, bf16[768,2048]{1,0:T(8,128)(2,1)}) custom-call(s32[1]{0:T(128)S(6)} %select_n.12.c_ref, f32[2048,768]{1,0:T(8,128)} %shard_map.212.h_ref, bf16[2048,768]{1,0:T(8,128)(2,1)} %y_ref.1, bf16[3,768,3072]{2,1,0:T(8,128)(2,1)} %convert_element_type.33.w1_hbm, ...), custom_call_target="tpu_custom_call" | custom-call | flops 115964116992 | bytes 97517568 | tf_op jit(solution)/shard_map/pallas_call | solution.py:153
  200.5 31.1 %dwi.1 = (bf16[1536,768]{1,0:T(8,128)(2,1)}, bf16[1536,768]{1,0:T(8,128)(2,1)}, bf16[1536,768]{1,0:T(8,128)(2,1)}, bf16[1536,768]{1,0:T(8,128)(2,1)}) custom-call(s32[1]{0:T(128)} %bitcast.i_ref.refs_0_, bf16[768,2048]{1,0:T(8,128)(2,1)} %get-tuple-element.65.g_ref, bf16[2048,6144]{1,0:T(8,128)(2,1)} %x_ref.3), custom_call_target="tpu_custom_call" | custom-call | flops 19327352832 | bytes 37748736 | tf_op jit(solution)/shard_map/dwi/pallas_call | solution.py:232
  231.5 2.0 collective-permute-start.1
  233.5 0.1 collective-permute-start.2
  233.6 0.0 collective-permute-done.4.y_ref
  233.6 0.0 collective-permute-done.3.h_ref
  233.6 141.8 %shard_map.214 = (bf16[2,3,3,768,2048]{4,3,2,1,0:T(8,128)(2,1)}, bf16[2,3,3,2048,768]{4,3,2,1,0:T(8,128)(2,1)}, bf16[768,2048]{1,0:T(8,128)(2,1)}) custom-call(s32[1]{0:T(128)S(6)} %select_n.12.c_ref, f32[2048,768]{1,0:T(8,128)} %collective-permute-done.3.h_ref, ...), custom_call_target="tpu_custom_call", output_to_operand_aliasing={{0}: (5, {}), {1}: (6, {})} | custom-call | flops 115964116992 | bytes 97517568 | tf_op jit(solution)/shard_map/pallas_call | solution.py:153
  375.4 0.0 collective-permute-done.1
  375.4 0.0 collective-permute-done.2
  375.4 6.3 add_convert_fusion.refs_4_
  381.8 28.5 %shard_map.216 = f32[4,768,768]{2,1,0:T(8,128)} custom-call(s32[1]{0:T(128)S(6)} %select_n.13.i_ref, bf16[2,3,3,768,2048]{4,3,2,1,0:T(8,128)(2,1)} %get-tuple-element.87.t_ref, bf16[2,3,3,2048,768]{4,3,2,1,0:T(8,128)(2,1)} %get-tuple-element.88.p_ref), custom_call_target="tpu_custom_call" | custom-call | flops 19327352832 | bytes 59768832 | tf_op jit(solution)/shard_map/pallas_call | solution.py:198
  410.2 0.1 collective-permute-start.8
  410.4 28.5 %shard_map.218 = f32[4,768,768]{2,1,0:T(8,128)} custom-call(s32[1]{0:T(128)S(6)} %select_n.13.i_ref, bf16[2,3,3,768,2048]{4,3,2,1,0:T(8,128)(2,1)} %get-tuple-element.87.t_ref, bf16[2,3,3,2048,768]{4,3,2,1,0:T(8,128)(2,1)} %get-tuple-element.88.p_ref), custom_call_target="tpu_custom_call" | custom-call | flops 19327352832 | bytes 59768832 | tf_op jit(solution)/shard_map/pallas_call | solution.py:198
  438.8 0.4 collective-permute-start.13
  439.2 0.0 collective-permute-done.8
  439.2 5.7 fusion.2.refs_7_
  444.9 28.7 %shard_map.217 = f32[4,768,768]{2,1,0:T(8,128)} custom-call(s32[1]{0:T(128)S(6)} %select_n.13.i_ref, bf16[2,3,3,768,2048]{4,3,2,1,0:T(8,128)(2,1)} %get-tuple-element.87.t_ref, bf16[2,3,3,2048,768]{4,3,2,1,0:T(8,128)(2,1)} %get-tuple-element.88.p_ref), custom_call_target="tpu_custom_call" | custom-call | flops 19327352832 | bytes 59768832 | tf_op jit(solution)/shard_map/pallas_call | solution.py:198
  473.5 0.1 collective-permute-start.9
  473.7 1.9 collective-permute-start.6
  475.6 0.2 collective-permute-start.18
  475.8 52.2 %collective-permute-done.6.refs_6_ = bf16[1536,768]{1,0:T(8,128)(2,1)S(1)} collective-permute-done((bf16[1536,768]{1,0:T(8,128)(2,1)}, bf16[1536,768]{1,0:T(8,128)(2,1)S(1)}, u32[]{:S(2)}, u32[]{:S(2)}) %collective-permute-start.6) | collective-permute-done | bytes 2359328 | tf_op jit(solution)/shard_map/ppermute | solution.py:696
  528.0 0.0 collective-permute-start.7
  528.0 0.0 collective-permute-done.13
  528.0 6.5 fusion.refs_7_
  534.5 1.9 collective-permute-start.15
  536.4 0.0 collective-permute-done.9
  536.4 1.9 fusion.1.refs_7_
  538.3 0.2 collective-permute-start.11
  538.5 40.2 %collective-permute-done.18.refs_9_ = bf16[2,768,768]{2,1,0:T(8,128)(2,1)} collective-permute-done((bf16[2,768,768]{2,1,0:T(8,128)(2,1)}, bf16[2,768,768]{2,1,0:T(8,128)(2,1)}, u32[]{:S(2)}, u32[]{:S(2)}) %collective-permute-start.18) | collective-permute-done | bytes 2359328 | tf_op jit(solution)/shard_map/ppermute | solution.py:696
  578.7 0.0 collective-permute-start.19
  578.7 0.0 collective-permute-done.7.refs_7_
  578.7 0.5 collective-permute-start.14
  579.2 50.0 %collective-permute-done.15.refs_9_ = bf16[2,768,768]{2,1,0:T(8,128)(2,1)} collective-permute-done((bf16[2,768,768]{2,1,0:T(8,128)(2,1)}, bf16[2,768,768]{2,1,0:T(8,128)(2,1)}, u32[]{:S(2)}, u32[]{:S(2)}) %collective-permute-start.15) | collective-permute-done | bytes 2359328 | tf_op jit(solution)/shard_map/ppermute | solution.py:696
  629.2 0.5 collective-permute-start.10
  629.8 49.4 %collective-permute-done.11.refs_9_ = bf16[2,768,768]{2,1,0:T(8,128)(2,1)} collective-permute-done((bf16[2,768,768]{2,1,0:T(8,128)(2,1)}, bf16[2,768,768]{2,1,0:T(8,128)(2,1)}, u32[]{:S(2)}, u32[]{:S(2)}) %collective-permute-start.11) | collective-permute-done | bytes 2359328 | tf_op jit(solution)/shard_map/ppermute | solution.py:696
  679.2 43.8 %shard_map.215 = (f32[6144,768]{1,0:T(8,128)}, f32[6144,768]{1,0:T(8,128)}, f32[6144,768]{1,0:T(8,128)}, bf16[6144,768]{1,0:T(8,128)(2,1)}) custom-call(s32[1]{0:T(128)} %bitcast.i_ref.refs_0_, f32[6144,768]{1,0:T(8,128)} %refs_1_.4, f32[6144,768]{1,0:T(8,128)} %refs_2_.4, f32[6144,768]{1,0:T(8,128)} %refs_3_.4, bf16[1536,768]{1,0:T(8,128)(2,1)} %add_convert_fusion.refs_4_, ...), custom_call_target="tpu_custom_call" | custom-call | flops 5662310400 | bytes 132120576 | tf_op jit(solution)/shard_map/pallas_call | solution.py:601
  723.0 60.4 %shard_map.219 = (f32[3,768,3072]{2,1,0:T(8,128)}, f32[3,768,3072]{2,1,0:T(8,128)}, f32[3,768,3072]{2,1,0:T(8,128)}, f32[3,3072,768]{2,1,0:T(8,128)}, f32[3,3072...) custom-call(s32[1]{0:T(128)} %bitcast.i_ref.refs_0_, ...), custom_call_target="tpu_custom_call" | custom-call | flops 5662310400 | bytes 132120576 | tf_op jit(solution)/shard_map/pallas_call | solution.py:601
  783.4 64.5 %shard_map.220 = (f32[3,768,3072]{2,1,0:T(8,128)}, f32[3,768,3072]{2,1,0:T(8,128)}, f32[3,768,3072]{2,1,0:T(8,128)}, f32[3,3072,768]{2,1,0:T(8,128)}, f32[3,3072...) custom-call(s32[1]{0:T(128)} %bitcast.i_ref.refs_0_, ...), custom_call_target="tpu_custom_call", output_to_operand_aliasing={{0}: (14, {}), {1}: (15, {}), {2}: (16, {}), {3}: (17, {}),... | custom-call | flops 5662310400 | bytes 132120576 | tf_op jit(solution)/shard_map/pallas_call | solution.py:601
  848.0 64.5 %shard_map.221 = (f32[3,768,3072]{2,1,0:T(8,128)}, f32[3,768,3072]{2,1,0:T(8,128)}, f32[3,768,3072]{2,1,0:T(8,128)}, f32[3,3072,768]{2,1,0:T(8,128)}, f32[3,3072...) custom-call(s32[1]{0:T(128)} %bitcast.i_ref.refs_0_, ...), custom_call_target="tpu_custom_call", output_to_operand_aliasing={{0}: (14, {}), {1}: (15, {}), {2}: (16, {}), {3}: (17, {}),... | custom-call | flops 5662310400 | bytes 132120576 | tf_op jit(solution)/shard_map/pallas_call | solution.py:601
  912.5 27.0 %last.1 = f32[2048,768]{1,0:T(8,128)} custom-call(f32[2048,768]{1,0:T(8,128)} %get-tuple-element.116.h_ref, bf16[4,768,768]{2,1,0:T(8,128)(2,1)} %bitcast.13, bf16[4,768,768]{2,1,0:T(8,128)(2,1)} %bitcast.14), custom_call_target="tpu_custom_call" | custom-call | flops 19327352832 | bytes 22020096 | tf_op jit(solution)/shard_map/last/pallas_call | solution.py:664
  939.6 4.6 multiply_reduce_fusion
  944.2 0.6 broadcast_multiply_fusion
  (24 shorter events, 0.1 us)
Async XLA Ops:
  0.6 233.0 %collective-permute-start.4 = (bf16[2048,768]{1,0:T(8,128)(2,1)}, bf16[2048,768]{1,0:T(8,128)(2,1)}, u32[]{:S(2)}, u32[]{:S(2)}) collective-permute-start(bf16[2048,768]{1,0:T(8,128)(2,1)} %y_ref.1), channel_id=1, source_target_pairs={{0,2},{2,0},{1,3},{3,1},{4,6},{6,4},{5,7},{7,5}} | collective-permute-start | bytes 9437192 | tf_op jit(solution)/shard_map/ppermute | solution.py:696
  30.9 202.8 %collective-permute-start.3 = (f32[2048,768]{1,0:T(8,128)}, f32[2048,768]{1,0:T(8,128)}, u32[]{:S(2)}, u32[]{:S(2)}) collective-permute-start(f32[2048,768]{1,0:T(8,128)} %shard_map.212.h_ref), channel_id=1, source_target_pairs={{0,2},{2,0},{1,3},{3,1},{4,6},{6,4},{5,7},{7,5}} | collective-permute-start | bytes 18874376 | tf_op jit(solution)/shard_map/ppermute | solution.py:696
  30.9 22.3 %copy-start = (f32[3,3072,768]{2,1,0:T(8,128)S(1)}, f32[3,3072,768]{2,1,0:T(8,128)}, u32[]{:S(2)}) copy-start(f32[3,3072,768]{2,1,0:T(8,128)} %refs_4_.5) | copy-start | bytes 84934656
  231.5 143.9 %collective-permute-start = (bf16[1536,768]{1,0:T(8,128)(2,1)}, bf16[1536,768]{1,0:T(8,128)(2,1)}, u32[]{:S(2)}, u32[]{:S(2)}) collective-permute-start(bf16[1536,768]{1,0:T(8,128)(2,1)} %get-tuple-element.67), channel_id=1, source_target_pairs={{0,1},{1,0},{2,3},{3,2},{4,5},{5,4},{6,7},{7,6}} | collective-permute-start | bytes 7077896 | tf_op jit(solution)/shard_map/ppermute | solution.py:696
  231.5 143.9 %collective-permute-start.1 = (bf16[1536,768]{1,0:T(8,128)(2,1)}, bf16[1536,768]{1,0:T(8,128)(2,1)}, u32[]{:S(2)}, u32[]{:S(2)}) collective-permute-start(bf16[1536,768]{1,0:T(8,128)(2,1)} %get-tuple-element.68), channel_id=1, source_target_pairs={{0,2},{2,0},{1,3},{3,1},{4,6},{6,4},{5,7},{7,5}} | collective-permute-start | bytes 7077896 | tf_op jit(solution)/shard_map/ppermute | solution.py:696
  233.5 141.9 %collective-permute-start.2 = (bf16[1536,768]{1,0:T(8,128)(2,1)}, bf16[1536,768]{1,0:T(8,128)(2,1)}, u32[]{:S(2)}, u32[]{:S(2)}) collective-permute-start(bf16[1536,768]{1,0:T(8,128)(2,1)} %get-tuple-element.69), channel_id=1, source_target_pairs={{0,3},{3,0},{1,2},{2,1},{4,7},{7,4},{5,6},{6,5}} | collective-permute-start | bytes 7077896 | tf_op jit(solution)/shard_map/ppermute | solution.py:696
  410.2 29.0 %collective-permute-start.8 = (f32[4,768,768]{2,1,0:T(8,128)}, f32[4,768,768]{2,1,0:T(8,128)}, u32[]{:S(2)}, u32[]{:S(2)}) collective-permute-start(f32[4,768,768]{2,1,0:T(8,128)} %shard_map.216), channel_id=1, source_target_pairs={{0,1},{1,0},{2,3},{3,2},{4,5},{5,4},{6,7},{7,6}} | collective-permute-start | bytes 28311560 | tf_op jit(solution)/shard_map/ppermute | solution.py:696
  438.8 89.2 %collective-permute-start.13 = (f32[4,768,768]{2,1,0:T(8,128)}, f32[4,768,768]{2,1,0:T(8,128)}, u32[]{:S(2)}, u32[]{:S(2)}) collective-permute-start(f32[4,768,768]{2,1,0:T(8,128)} %shard_map.218), channel_id=1, source_target_pairs={{0,1},{1,0},{2,3},{3,2},{4,5},{5,4},{6,7},{7,6}} | collective-permute-start | bytes 28311560 | tf_op jit(solution)/shard_map/ppermute | solution.py:696
  473.5 62.8 %copy-start.2 = (bf16[2,768,768]{2,1,0:T(8,128)(2,1)S(1)}, bf16[2,768,768]{2,1,0:T(8,128)(2,1)}, u32[]{:S(2)}) copy-start(bf16[2,768,768]{2,1,0:T(8,128)(2,1)} %fusion.2.refs_7_) | copy-start | bytes 7077892
  473.5 62.8 %copy-start.1 = (f32[4,768,768]{2,1,0:T(8,128)S(1)}, f32[4,768,768]{2,1,0:T(8,128)}, u32[]{:S(2)}) copy-start(f32[4,768,768]{2,1,0:T(8,128)} %shard_map.217) | copy-start | bytes 28311556
  473.5 62.8 %collective-permute-start.9 = (f32[4,768,768]{2,1,0:T(8,128)}, f32[4,768,768]{2,1,0:T(8,128)S(1)}, u32[]{:S(2)}, u32[]{:S(2)}) collective-permute-start(f32[4,768,768]{2,1,0:T(8,128)} %shard_map.217), channel_id=1, source_target_pairs={{0,1},{1,0},{2,3},{3,2},{4,5},{5,4},{6,7},{7,6}} | collective-permute-start | bytes 28311560 | tf_op jit(solution)/shard_map/ppermute | solution.py:696
  473.7 54.3 %collective-permute-start.6 = (bf16[1536,768]{1,0:T(8,128)(2,1)}, bf16[1536,768]{1,0:T(8,128)(2,1)S(1)}, u32[]{:S(2)}, u32[]{:S(2)}) collective-permute-start(bf16[1536,768]{1,0:T(8,128)(2,1)} %add_convert_fusion.refs_4_), channel_id=1, source_target_pairs={{0,2},{2,0},{1,3},{3,1},{4,6},{6,4},{5,7},{7,5}} | collective-permute-start | bytes 7077896 | tf_op jit(solution)/shard_map/ppermute | solution.py:696
  475.6 62.7 %collective-permute-start.5 = (bf16[1536,768]{1,0:T(8,128)(2,1)}, bf16[1536,768]{1,0:T(8,128)(2,1)S(1)}, u32[]{:S(2)}, u32[]{:S(2)}) collective-permute-start(bf16[1536,768]{1,0:T(8,128)(2,1)} %add_convert_fusion.refs_4_), channel_id=1, source_target_pairs={{0,1},{1,0},{2,3},{3,2},{4,5},{5,4},{6,7},{7,6}} | collective-permute-start | bytes 7077896 | tf_op jit(solution)/shard_map/ppermute | solution.py:696
  475.6 103.1 %collective-permute-start.18 = (bf16[2,768,768]{2,1,0:T(8,128)(2,1)}, bf16[2,768,768]{2,1,0:T(8,128)(2,1)}, u32[]{:S(2)}, u32[]{:S(2)}) collective-permute-start(bf16[2,768,768]{2,1,0:T(8,128)(2,1)} %fusion.2.refs_7_), channel_id=1, source_target_pairs={{0,2},{2,0},{1,3},{3,1},{4,6},{6,4},{5,7},{7,5}} | collective-permute-start | bytes 7077896 | tf_op jit(solution)/shard_map/ppermute | solution.py:696
  528.0 10.3 %copy-start.3 = (bf16[1536,768]{1,0:T(8,128)(2,1)}, bf16[1536,768]{1,0:T(8,128)(2,1)S(1)}, u32[]{:S(2)}) copy-start(bf16[1536,768]{1,0:T(8,128)(2,1)S(1)} %collective-permute-done.6.refs_6_) | copy-start | bytes 7077892
  528.0 50.7 %collective-permute-start.7 = (bf16[1536,768]{1,0:T(8,128)(2,1)S(1)}, bf16[1536,768]{1,0:T(8,128)(2,1)S(1)}, u32[]{:S(2)}, u32[]{:S(2)}) collective-permute-start(bf16[1536,768]{1,0:T(8,128)(2,1)S(1)} %collective-permute-done.6.refs_6_), channel_id=1, source_target_pairs={{0,1},{1,0},{2,3},{3,2},{4,5},{5,4},{6,7},{7,6}} | collective-permute-start | bytes 7077896 | tf_op jit(solution)/shard_map/ppermute | solution.py:696
  534.5 94.8 %collective-permute-start.15 = (bf16[2,768,768]{2,1,0:T(8,128)(2,1)}, bf16[2,768,768]{2,1,0:T(8,128)(2,1)}, u32[]{:S(2)}, u32[]{:S(2)}) collective-permute-start(bf16[2,768,768]{2,1,0:T(8,128)(2,1)} %fusion.refs_7_), channel_id=1, source_target_pairs={{0,2},{2,0},{1,3},{3,1},{4,6},{6,4},{5,7},{7,5}} | collective-permute-start | bytes 7077896 | tf_op jit(solution)/shard_map/ppermute | solution.py:696
  536.4 92.9 %collective-permute-start.17 = (bf16[2,768,768]{2,1,0:T(8,128)(2,1)S(1)}, bf16[2,768,768]{2,1,0:T(8,128)(2,1)}, u32[]{:S(2)}, u32[]{:S(2)}) collective-permute-start(bf16[2,768,768]{2,1,0:T(8,128)(2,1)S(1)} %copy-done.2), channel_id=1, source_target_pairs={{0,1},{1,0},{2,3},{3,2},{4,5},{5,4},{6,7},{7,6}} | collective-permute-start | bytes 7077896 | tf_op jit(solution)/shard_map/ppermute | solution.py:696
  538.3 91.0 %copy-start.4 = (bf16[1536,768]{1,0:T(8,128)(2,1)}, bf16[1536,768]{1,0:T(8,128)(2,1)S(1)}, u32[]{:S(2)}) copy-start(bf16[1536,768]{1,0:T(8,128)(2,1)S(1)} %collective-permute-done.5.refs_5_) | copy-start | bytes 7077892
  538.3 140.9 %collective-permute-start.11 = (bf16[2,768,768]{2,1,0:T(8,128)(2,1)}, bf16[2,768,768]{2,1,0:T(8,128)(2,1)}, u32[]{:S(2)}, u32[]{:S(2)}) collective-permute-start(bf16[2,768,768]{2,1,0:T(8,128)(2,1)} %fusion.1.refs_7_), channel_id=1, source_target_pairs={{0,2},{2,0},{1,3},{3,1},{4,6},{6,4},{5,7},{7,5}} | collective-permute-start | bytes 7077896 | tf_op jit(solution)/shard_map/ppermute | solution.py:696
  578.7 144.4 %collective-permute-start.19 = (bf16[2,768,768]{2,1,0:T(8,128)(2,1)}, bf16[2,768,768]{2,1,0:T(8,128)(2,1)}, u32[]{:S(2)}, u32[]{:S(2)}) collective-permute-start(bf16[2,768,768]{2,1,0:T(8,128)(2,1)} %collective-permute-done.18.refs_9_), channel_id=1, source_target_pairs={{0,1},{1,0},{2,3},{3,2},{4,5},{5,4},{6,7},{7,6}} | collective-permute-start | bytes 7077896 | tf_op jit(solution)/shard_map/ppermute | solution.py:696
  578.7 51.1 %copy-start.5 = (bf16[1536,768]{1,0:T(8,128)(2,1)}, bf16[1536,768]{1,0:T(8,128)(2,1)S(1)}, u32[]{:S(2)}) copy-start(bf16[1536,768]{1,0:T(8,128)(2,1)S(1)} %collective-permute-done.7.refs_7_) | copy-start | bytes 7077892
  578.7 204.7 %collective-permute-start.14 = (bf16[2,768,768]{2,1,0:T(8,128)(2,1)}, bf16[2,768,768]{2,1,0:T(8,128)(2,1)}, u32[]{:S(2)}, u32[]{:S(2)}) collective-permute-start(bf16[2,768,768]{2,1,0:T(8,128)(2,1)} %fusion.refs_7_), channel_id=1, source_target_pairs={{0,1},{1,0},{2,3},{3,2},{4,5},{5,4},{6,7},{7,6}} | collective-permute-start | bytes 7077896 | tf_op jit(solution)/shard_map/ppermute | solution.py:696
  629.2 154.2 %collective-permute-start.16 = (bf16[2,768,768]{2,1,0:T(8,128)(2,1)}, bf16[2,768,768]{2,1,0:T(8,128)(2,1)}, u32[]{:S(2)}, u32[]{:S(2)}) collective-permute-start(bf16[2,768,768]{2,1,0:T(8,128)(2,1)} %collective-permute-done.15.refs_9_), channel_id=1, source_target_pairs={{0,1},{1,0},{2,3},{3,2},{4,5},{5,4},{6,7},{7,6}} | collective-permute-start | bytes 7077896 | tf_op jit(solution)/shard_map/ppermute | solution.py:696
  629.2 218.7 %collective-permute-start.10 = (bf16[2,768,768]{2,1,0:T(8,128)(2,1)}, bf16[2,768,768]{2,1,0:T(8,128)(2,1)}, u32[]{:S(2)}, u32[]{:S(2)}) collective-permute-start(bf16[2,768,768]{2,1,0:T(8,128)(2,1)} %fusion.1.refs_7_), channel_id=1, source_target_pairs={{0,1},{1,0},{2,3},{3,2},{4,5},{5,4},{6,7},{7,6}} | collective-permute-start | bytes 7077896 | tf_op jit(solution)/shard_map/ppermute | solution.py:696
  679.2 168.8 %collective-permute-start.12 = (bf16[2,768,768]{2,1,0:T(8,128)(2,1)}, bf16[2,768,768]{2,1,0:T(8,128)(2,1)}, u32[]{:S(2)}, u32[]{:S(2)}) collective-permute-start(bf16[2,768,768]{2,1,0:T(8,128)(2,1)} %collective-permute-done.11.refs_9_), channel_id=1, source_target_pairs={{0,1},{1,0},{2,3},{3,2},{4,5},{5,4},{6,7},{7,6}} | collective-permute-start | bytes 7077896 | tf_op jit(solution)/shard_map/ppermute | solution.py:696
